TPU v7x, 128 devices: a whole 4x4x4 slice. The times are simulated.
128 devices in a mesh: tm: 64 (over z, y, x_lo, core), space: 2 (over x_hi).
Axes of the slice: x: 4 (x_hi: 2, x_lo: 2; x = x_hi * 2 + x_lo), y: 4, z: 4, core: 2. Of those that a mesh axis runs over, the one named last changes fastest.
Arguments:
- u_init: float32 [2, 512, 512], P(None, 'space'), may hold values from -8 to 8
- phase: float32 [512, 512], P('space'), may hold values from 0.005 to 0.05
- absorb: float32 [512, 512], P('space'), may hold values from 0.004 to 0.04
Outputs:
- solution: float32 [2, 64, 512, 512], P(None, 'tm', 'space')
All inputs are finite; a program needn't handle non-finite values.
Results may differ from a plain program's by a relative error of at most 0.0003.
Values sent between devices are 32-bit elements; how exact they have to be, the bound alone decides.
No kernel may reach another device: no remote copies, remote signals or barrier semaphores. Data moves between devices by JAX's collectives and lax.ppermute only.
A program may use at most 192 MiB of HBM per device.

v0:
```python
import functools
import math

import jax
import jax.numpy as jnp
from jax import lax
from jax.sharding import Mesh
from jax.sharding import PartitionSpec as P

NX = 512
NY = 512
TS_DEV = 1
ITERS = 4
TM = ("tm_0", "tm_1", "tm_2", "tm_3")
TM_SPACE = ("tm_0", "tm_1", "tm_2", "tm_3", "space")


tau = 400.0
alpha = 0.4
highest = lax.Precision.HIGHEST


def with_halo(cells, sides, width):
    for axis, dim in sides:
        count = lax.axis_size(axis)
        head = lax.slice_in_dim(cells, 0, width, axis=dim)
        tail = lax.slice_in_dim(cells, cells.shape[dim] - width, cells.shape[dim], axis=dim)
        cells = jnp.concatenate(
            [
                lax.ppermute(tail, axis, [(i, (i + 1) % count) for i in range(count)]),
                cells,
                lax.ppermute(head, axis, [((i + 1) % count, i) for i in range(count)]),
            ],
            axis=dim,
        )
    return cells


def shifted(value, axis, steps):
    count = lax.axis_size(axis)
    leading, last = (max(0, -steps), min(count, count - steps))
    return lax.ppermute(value, axis, [(source, source + steps) for source in range(leading, last)])


def in_blocks(value, dim, count):
    before, after = (value.shape[:dim], value.shape[dim + 1 :])
    return jnp.moveaxis(value.reshape(*before, count, -1, *after), dim, 0)


def piece_ends(length, count):
    hop = length // count
    if hop >= 8:
        hop -= hop % 8
    return [hop * k for k in range(1, count)]


def in_order(parts, dim):
    parts = jnp.moveaxis(parts, 0, dim)
    shape = parts.shape
    return parts.reshape(*shape[:dim], shape[dim] * shape[dim + 1], *shape[dim + 2 :])


def exchange_in_pieces(value, axis, pieces, split_dim, concat_dim):
    parts = in_blocks(value, split_dim, lax.axis_size(axis))
    cut = max(range(1, max(2, parts.ndim - 1)), key=lambda d: parts.shape[d])
    done = []
    for piece in jnp.split(parts, piece_ends(parts.shape[cut], pieces), axis=cut):
        if piece.size:
            done.append(lax.all_to_all(piece, axis, split_axis=0, concat_axis=0, tiled=True))
    return in_order(jnp.concatenate(done, axis=cut), concat_dim)


def by_axis(value, axes):
    return functools.reduce(lax.psum, axes, value)


def tables(length):
    index = jnp.arange(length, dtype=jnp.int32)
    product = index[:, None] * index[None, :] % length
    angle = product.astype(jnp.float32) * (2.0 * math.pi / length)
    return (jnp.cos(angle), jnp.sin(angle))


def mix(field, cosine, sine, sign, pattern):
    real_part = jnp.einsum(pattern, field[0], cosine, precision=highest) - sign * jnp.einsum(
        pattern, field[1], sine, precision=highest
    )
    imag_part = jnp.einsum(pattern, field[1], cosine, precision=highest) + sign * jnp.einsum(
        pattern, field[0], sine, precision=highest
    )
    return jnp.stack([real_part, imag_part])


def laplacian(field):
    padded = with_halo(field, (("space", 2),), 1)
    return (
        padded[:, :, 2:]
        + padded[:, :, :-2]
        + jnp.roll(field, 1, 3)
        + jnp.roll(field, -1, 3)
        - 4.0 * field
    )


def generator(field, phase, absorb):
    curvature = laplacian(field)
    change_real = -tau * curvature[1] + phase * field[1] - absorb * field[0]
    change_imag = tau * curvature[0] - phase * field[0] - absorb * field[1]
    return jnp.stack([change_real, change_imag])


def operate(field, phase, absorb):
    change = generator(field, phase, absorb)
    ahead = field + 0.5 * change
    behind = field - 0.5 * change
    earlier = shifted(ahead, TM, 1)
    previous = jnp.concatenate([earlier, ahead[:, :-1]], axis=1)
    return behind - previous


def first_mode(block):
    return (lax.axis_index(TM) * lax.axis_size("space") + lax.axis_index("space")) * block


def least_squares(hessenberg, start):
    matrix = [list(line) for line in hessenberg]
    target = [start] + [jnp.zeros((), jnp.float32) for unused in range(ITERS)]
    cosines = []
    sines = []
    for column in range(ITERS):
        for row in range(column):
            upper = matrix[row][column]
            lower = matrix[row + 1][column]
            matrix[row][column] = cosines[row] * upper + sines[row] * lower
            matrix[row + 1][column] = -sines[row] * upper + cosines[row] * lower
        upper = matrix[column][column]
        lower = matrix[column + 1][column]
        radius = jnp.sqrt(upper * upper + lower * lower)
        cosines.append(upper / radius)
        sines.append(lower / radius)
        matrix[column][column] = radius
        target[column + 1] = -sines[column] * target[column]
        target[column] = cosines[column] * target[column]
    factors = [None] * ITERS
    for row in reversed(range(ITERS)):
        total = target[row]
        for other in range(row + 1, ITERS):
            total = total - matrix[row][other] * factors[other]
        factors[row] = total / matrix[row][row]
    return factors


def shards(u_init, phase, absorb):
    parts_time = lax.axis_size(TM)
    parts_space = lax.axis_size("space")
    steps_all = parts_time * TS_DEV
    rows_here = NX // parts_space
    block = NY // (parts_time * parts_space)
    row_cosine, row_sine = tables(NX)
    column_cosine, column_sine = tables(NY)
    time_cosine, time_sine = tables(steps_all)
    beta = jnp.float32(alpha) ** (1.0 / steps_all)
    frequency = jnp.arange(steps_all).astype(jnp.float32) * (2.0 * math.pi / steps_all)
    cosine = (beta * jnp.cos(frequency))[None, :, None]
    sine = (beta * jnp.sin(frequency))[None, :, None]
    modes_y = (first_mode(block) + jnp.arange(block, dtype=jnp.int32)).astype(jnp.float32)
    symbol_y = 4.0 * jnp.sin(modes_y * (math.pi / NY)) ** 2
    symbol_x = 4.0 * jnp.sin(jnp.arange(NX).astype(jnp.float32) * (math.pi / NX)) ** 2
    symbol = symbol_y[:, None, None] + symbol_x[None, None, :]
    eigen_real = 1.0 - cosine + tau * symbol * sine / 2.0
    eigen_imag = sine + tau * symbol * (1.0 + cosine) / 2.0
    modulus = eigen_real * eigen_real + eigen_imag * eigen_imag
    ratio_real = eigen_real / modulus
    ratio_imag = eigen_imag / modulus
    step_index = lax.axis_index(TM) * TS_DEV + jnp.arange(TS_DEV, dtype=jnp.int32)
    weights = jnp.float32(alpha) ** (step_index.astype(jnp.float32) / steps_all)
    start_field = u_init[:, None]
    first = start_field + 0.5 * generator(start_field, phase, absorb)
    right_side = jnp.where((step_index == 0)[None, :, None, None], first, 0.0)
    corrected = []
    hessenberg = [
        [jnp.zeros((), jnp.float32) for unused in range(ITERS)] for other in range(ITERS + 1)
    ]
    basis = []
    pending = right_side
    start = None
    for column in range(ITERS):
        weighted = pending * weights[None, :, None, None]
        spread = mix(weighted, column_cosine, column_sine, -1.0, "trc,kc->ktr")
        flat = spread.reshape(2, NY, TS_DEV * rows_here)
        arrived = lax.all_to_all(flat, TM_SPACE, split_axis=1, concat_axis=2, tiled=True)
        arrived = arrived.reshape(2, block, parts_time, parts_space, TS_DEV, rows_here)
        arrived = arrived.transpose(0, 1, 2, 4, 3, 5).reshape(2, block, steps_all, NX)
        modes = mix(arrived, row_cosine, row_sine, -1.0, "ytr,kr->ytk")
        spectrum = mix(modes, time_cosine, time_sine, -1.0, "ytx,kt->ykx")
        solved = jnp.stack(
            [
                spectrum[0] * ratio_real + spectrum[1] * ratio_imag,
                spectrum[1] * ratio_real - spectrum[0] * ratio_imag,
            ]
        )
        timed = mix(solved, time_cosine, time_sine, 1.0, "ykx,tk->ytx") / steps_all
        spatial = mix(timed, row_cosine, row_sine, 1.0, "ytk,rk->ytr") / NX
        spatial = spatial.reshape(2, block, parts_time, TS_DEV, parts_space, rows_here)
        spatial = spatial.transpose(0, 1, 2, 4, 3, 5).reshape(2, block, steps_all * NX)
        returned = exchange_in_pieces(spatial, TM_SPACE, 2, 2, 1)
        returned = returned.reshape(2, NY, TS_DEV, rows_here)
        result = mix(returned, column_cosine, column_sine, 1.0, "ktr,ck->trc") / NY
        raw_update = result / weights[None, :, None, None]
        raw_image = operate(raw_update, phase, absorb)
        partial_value = tuple(
            (
                jnp.sum(raw_image * basis[row]) if row < column else jnp.zeros((), jnp.float32)
                for row in range(ITERS - 1)
            )
        )
        totals = jax.tree.map(
            lambda part: by_axis(part, TM_SPACE),
            partial_value + (jnp.sum(raw_image * pending), jnp.sum(pending * pending)),
        )
        length = jnp.sqrt(totals[-1])
        if column == 0:
            start = length
        else:
            hessenberg[column][column - 1] = length
        basis.append(pending / length)
        update = raw_update / length
        corrected.append(update)
        image = raw_image / length
        products = [totals[row] / length for row in range(column)]
        products.append(totals[-2] / (length * length))
        for vector, amount in zip(basis, products):
            image = image - amount * vector
        for row in range(column + 1):
            hessenberg[row][column] = products[row]
        pending = image
    hessenberg[ITERS][ITERS - 1] = jnp.sqrt(by_axis(jnp.sum(pending * pending), TM_SPACE))
    factors = least_squares(hessenberg, start)
    solution = jnp.zeros_like(right_side)
    for amount, update in zip(factors, corrected):
        solution = solution + amount * update
    return solution


def solution(mesh):
    torus = Mesh(
        mesh.devices.reshape(4, 4, 2, 2, mesh.shape["space"]),
        ("tm_0", "tm_1", "tm_2", "tm_3", "space"),
    )
    placed = (P(None, "space", None), P("space", None), P("space", None))
    return jax.shard_map(
        shards, mesh=torus, in_specs=placed, out_specs=P(None, TM, "space", None), check_vma=False
    )
```

profile of v0, /device:TPU:1, one launch (start us, length us, event | category | flops | bytes accessed | tf_op | source)
XLA Modules:
  0.0 1017.6 jit_solution(4753657251585213269)
XLA Ops:
  33.2 11.6 %all-to-all-start = ((f32[2,512,256]{2,0,1:T(2,128)}), f32[2,512,256]{2,0,1:T(2,128)S(1)}, u32[]{:S(2)}, u32[]{:S(2)}) async-start(f32[2,512,256]{2,0,1:T(2,128)} %copy.52), calls=%async_computation | async-start | bytes 2097152 | tf_op jit(solution)/shard_map/all_to_all | solution.py:191
  45.1 18.8 %all-to-all-done = f32[2,512,256]{2,0,1:T(2,128)S(1)} async-done(((f32[2,512,256]{2,0,1:T(2,128)}), f32[2,512,256]{2,0,1:T(2,128)S(1)}, u32[]{:S(2)}, u32[]{:S(2)}) %all-to-all-start) | async-done | bytes 1048608 | tf_op jit(solution)/shard_map/all_to_all | solution.py:191
  116.5 17.4 %all_to_all.100 = f32[128,2,2,256]{3,2,1,0:T(2,128)S(1)} all-to-all(f32[128,2,2,256]{3,2,1,0:T(2,128)S(1)} %get-tuple-element.152), channel_id=1, replica_groups=mesh['tm_0'=4,'tm_1'=4,'tm_2'=2,'tm_3'=2,'space'=2] {'tm_0','tm_1','tm_2..., dimensions={0} | all-to-all | bytes 1048576 | tf_op jit(solution)/shard_map/all_to_all | solution.py:69
  134.0 17.5 %all_to_all.101 = f32[128,2,2,256]{3,2,1,0:T(2,128)S(1)} all-to-all(f32[128,2,2,256]{3,2,1,0:T(2,128)S(1)} %get-tuple-element.153), channel_id=1, replica_groups=mesh['tm_0'=4,'tm_1'=4,'tm_2'=2,'tm_3'=2,'space'=2] {'tm_0','tm_1','tm_2..., dimensions={0} | all-to-all | bytes 1048576 | tf_op jit(solution)/shard_map/all_to_all | solution.py:69
  152.3 5.8 fusion.204
  158.3 5.8 fusion.202
  164.1 5.9 fusion.13
  170.0 6.3 fusion.12
  188.0 11.7 %collective-permute-done.4 = f32[2,1,256,512]{3,2,1,0:T(8,128)S(1)} collective-permute-done((f32[2,1,256,512]{3,2,1,0:T(8,128)S(1)}, f32[2,1,256,512]{3,2,1,0:T(8,128)S(1)}, u32[]{:S(2)}, u32[]{:S(2)}) %collective-permute-start.4) | collective-permute-done | bytes 1048608 | tf_op jit(solution)/shard_map/ppermute | solution.py:42
  200.9 7.3 all-reduce.7
  208.2 7.0 all-reduce.3
  220.7 11.4 %all-reduce.15 = (f32[]{:T(128)}, f32[]{:T(128)}) all-reduce(f32[]{:T(128)} %get-tuple-element.83, f32[]{:T(128)} %get-tuple-element.84), channel_id=1, replica_groups=mesh['tm_0'=4,'tm_1'=4,'tm_2'=2,'tm_3'=2,'space'=2] {'tm_3'}, use_global_device_ids=true, to_apply=%region_4.5 | all-reduce | flops 2 | bytes 16 | tf_op jit(solution)/shard_map/psum | solution.py:74
  232.1 6.2 all-reduce.11
  262.1 25.7 %all_to_all.102 = f32[2,512,256]{2,0,1:T(2,128)S(1)} all-to-all(f32[2,512,256]{2,0,1:T(2,128)S(1)} %copy.59), channel_id=1, replica_groups=mesh['tm_0'=4,'tm_1'=4,'tm_2'=2,'tm_3'=2,'space'=2] {'tm_0','tm_1','tm_2..., dimensions={1} | all-to-all | bytes 2097152 | tf_op jit(solution)/shard_map/all_to_all | solution.py:191
  289.2 6.9 convolution_multiply_fusion.8
  324.8 6.2 fusion.109
  337.3 6.7 convolution_add_fusion.9
  346.2 17.4 %all_to_all.103 = f32[128,2,2,256]{3,2,1,0:T(2,128)S(1)} all-to-all(f32[128,2,2,256]{3,2,1,0:T(2,128)S(1)} %get-tuple-element.140), channel_id=1, replica_groups=mesh['tm_0'=4,'tm_1'=4,'tm_2'=2,'tm_3'=2,'space'=2] {'tm_0','tm_1','tm_2..., dimensions={0} | all-to-all | bytes 1048576 | tf_op jit(solution)/shard_map/all_to_all | solution.py:69
  363.6 17.5 %all_to_all.104 = f32[128,2,2,256]{3,2,1,0:T(2,128)S(1)} all-to-all(f32[128,2,2,256]{3,2,1,0:T(2,128)S(1)} %get-tuple-element.141), channel_id=1, replica_groups=mesh['tm_0'=4,'tm_1'=4,'tm_2'=2,'tm_3'=2,'space'=2] {'tm_0','tm_1','tm_2..., dimensions={0} | all-to-all | bytes 1048576 | tf_op jit(solution)/shard_map/all_to_all | solution.py:69
  382.7 7.4 fusion.192
  396.2 5.9 fusion.9
  402.0 5.9 fusion.8
  419.6 11.7 %collective-permute-done.7 = f32[2,1,256,512]{3,2,1,0:T(8,128)S(1)} collective-permute-done((f32[2,1,256,512]{3,2,1,0:T(8,128)S(1)}, f32[2,1,256,512]{3,2,1,0:T(8,128)S(1)}, u32[]{:S(2)}, u32[]{:S(2)}) %collective-permute-start.7) | collective-permute-done | bytes 1048608 | tf_op jit(solution)/shard_map/ppermute | solution.py:42
  433.6 7.3 all-reduce.6
  440.9 7.0 all-reduce.2
  453.4 11.4 %all-reduce.14 = (f32[]{:T(128)}, f32[]{:T(128)}, f32[]{:T(128)}) all-reduce(f32[]{:T(128)} %get-tuple-element.80, f32[]{:T(128)} %get-tuple-element.81, f32[]{:T(128)} %get-tuple-element.82), channel_id=1, replica_groups=mesh['tm_0'=4,'tm_1'=4,'tm_2'=2,'tm_3'=2,'space'=2] {'tm_3'}, use_global_device_ids=true, to_apply=%region_28.29 | all-reduce | flops 3 | bytes 24 | tf_op jit(solution)/shard_map/psum | solution.py:74
  464.7 6.3 all-reduce.10
  495.0 25.5 %all_to_all.105 = f32[2,512,256]{2,0,1:T(2,128)S(1)} all-to-all(f32[2,512,256]{2,0,1:T(2,128)S(1)} %copy.68), channel_id=1, replica_groups=mesh['tm_0'=4,'tm_1'=4,'tm_2'=2,'tm_3'=2,'space'=2] {'tm_0','tm_1','tm_2..., dimensions={1} | all-to-all | bytes 2097152 | tf_op jit(solution)/shard_map/all_to_all | solution.py:191
  523.9 6.9 convolution_multiply_fusion.4
  532.7 6.0 convolution_multiply_fusion.5
  562.2 6.0 fusion.103
  578.2 6.7 convolution_add_fusion.5
  589.1 17.4 %all_to_all.106 = f32[128,2,2,256]{3,2,1,0:T(2,128)S(1)} all-to-all(f32[128,2,2,256]{3,2,1,0:T(2,128)S(1)} %get-tuple-element.128), channel_id=1, replica_groups=mesh['tm_0'=4,'tm_1'=4,'tm_2'=2,'tm_3'=2,'space'=2] {'tm_0','tm_1','tm_2..., dimensions={0} | all-to-all | bytes 1048576 | tf_op jit(solution)/shard_map/all_to_all | solution.py:69
  606.5 17.7 %all_to_all.107 = f32[128,2,2,256]{3,2,1,0:T(2,128)S(1)} all-to-all(f32[128,2,2,256]{3,2,1,0:T(2,128)S(1)} %get-tuple-element.129), channel_id=1, replica_groups=mesh['tm_0'=4,'tm_1'=4,'tm_2'=2,'tm_3'=2,'space'=2] {'tm_0','tm_1','tm_2..., dimensions={0} | all-to-all | bytes 1048576 | tf_op jit(solution)/shard_map/all_to_all | solution.py:69
  627.8 7.4 fusion.195
  637.2 6.7 fusion.197
  644.0 6.3 fusion.5
  650.3 5.9 fusion.4
  667.9 11.7 %collective-permute-done.10 = f32[2,1,256,512]{3,2,1,0:T(8,128)S(1)} collective-permute-done((f32[2,1,256,512]{3,2,1,0:T(8,128)S(1)}, f32[2,1,256,512]{3,2,1,0:T(8,128)S(1)}, u32[]{:S(2)}, u32[]{:S(2)}) %collective-permute-start.10) | collective-permute-done | bytes 1048608 | tf_op jit(solution)/shard_map/ppermute | solution.py:42
  681.9 7.3 all-reduce.5
  689.2 7.0 all-reduce.1
  701.7 11.4 %all-reduce.13 = (f32[]{:T(128)}, f32[]{:T(128)}, f32[]{:T(128)}, f32[]{:T(128)}) all-reduce(f32[]{:T(128)} %get-tuple-element.76, f32[]{:T(128)} %get-tuple-element.77, f32[]{:T(128)} %get-tuple-element.78, f32[]{:T(128)} %get-tuple-element.79), channel_id=1, replica_groups=mesh['tm_0'=4,'tm_1'=4,'tm_2'=2,'tm_3'=2,'space'=2] {'tm_3'}, use_global_device_ids=true, to_apply=%region_52.53 | all-reduce | flops 4 | bytes 32 | tf_op jit(solution)/shard_map/psum | solution.py:74
  713.1 6.1 all-reduce.9
  744.9 25.7 %all_to_all.108 = f32[2,512,256]{2,0,1:T(2,128)S(1)} all-to-all(f32[2,512,256]{2,0,1:T(2,128)S(1)} %copy.74), channel_id=1, replica_groups=mesh['tm_0'=4,'tm_1'=4,'tm_2'=2,'tm_3'=2,'space'=2] {'tm_0','tm_1','tm_2..., dimensions={1} | all-to-all | bytes 2097152 | tf_op jit(solution)/shard_map/all_to_all | solution.py:191
  774.0 6.9 convolution_multiply_fusion
  782.9 6.0 convolution_multiply_fusion.1
  812.1 6.0 fusion.97
  818.1 5.8 convolution_subtract_fusion.1
  828.2 6.8 convolution_add_fusion.1
  839.0 17.5 %all_to_all.109 = f32[128,2,2,256]{3,2,1,0:T(2,128)S(1)} all-to-all(f32[128,2,2,256]{3,2,1,0:T(2,128)S(1)} %get-tuple-element.116), channel_id=1, replica_groups=mesh['tm_0'=4,'tm_1'=4,'tm_2'=2,'tm_3'=2,'space'=2] {'tm_0','tm_1','tm_2..., dimensions={0} | all-to-all | bytes 1048576 | tf_op jit(solution)/shard_map/all_to_all | solution.py:69
  856.5 17.8 %all_to_all.110 = f32[128,2,2,256]{3,2,1,0:T(2,128)S(1)} all-to-all(f32[128,2,2,256]{3,2,1,0:T(2,128)S(1)} %get-tuple-element.117), channel_id=1, replica_groups=mesh['tm_0'=4,'tm_1'=4,'tm_2'=2,'tm_3'=2,'space'=2] {'tm_0','tm_1','tm_2..., dimensions={0} | all-to-all | bytes 1048576 | tf_op jit(solution)/shard_map/all_to_all | solution.py:69
  878.0 7.4 fusion.207
  887.4 6.7 fusion.209
  894.2 6.0 fusion.1
  900.2 5.9 fusion
  919.9 11.1 %collective-permute-done.13 = f32[2,1,256,512]{3,2,1,0:T(8,128)} collective-permute-done((f32[2,1,256,512]{3,2,1,0:T(8,128)}, f32[2,1,256,512]{3,2,1,0:T(8,128)}, u32[]{:S(2)}, u32[]{:S(2)}) %collective-permute-start.13) | collective-permute-done | bytes 1048608 | tf_op jit(solution)/shard_map/ppermute | solution.py:42
  935.1 7.3 all-reduce.4
  942.4 7.0 all-reduce
  954.9 11.4 %all-reduce.12 = (f32[]{:T(128)}, f32[]{:T(128)}, f32[]{:T(128)}, f32[]{:T(128)}, f32[]{:T(128)}) all-reduce(f32[]{:T(128)} %get-tuple-element.71, f32[]{:T(128)} %get-tuple-element.72, f32[]{:T(128)} %get-tuple-element.73, f32[]{:T(128)} %get-tuple-element.74, ...), channel_id=1, replica_groups=mesh['tm_0'=4,'tm_1'=4,'tm_2'=2,'tm_3'=2,'space'=2] {'tm_3'}, use_global_device_ids=true, to_apply=%region_58.59 | all-reduce | flops 5 | bytes 40 | tf_op jit(solution)/shard_map/psum | solution.py:74
  966.3 6.0 all-reduce.8
  978.4 6.6 psum.595
  985.1 8.3 psum.596
  998.1 8.8 psum.598
  1006.9 5.9 psum.599
  (325 shorter events, 381.6 us)
Async XLA Ops:
  0.8 7.6 collective-permute-start
  4.4 3.1 copy-start
  4.4 4.0 collective-permute-start.1
  8.4 1.9 copy-start.3
  8.4 1.9 copy-start.8
  33.2 30.7 %all-to-all-start = ((f32[2,512,256]{2,0,1:T(2,128)}), f32[2,512,256]{2,0,1:T(2,128)S(1)}, u32[]{:S(2)}, u32[]{:S(2)}) async-start(f32[2,512,256]{2,0,1:T(2,128)} %copy.52), calls=%async_computation | async-start | bytes 2097152 | tf_op jit(solution)/shard_map/all_to_all | solution.py:191
  70.4 5.3 copy-start.47
  94.0 10.0 copy-start.29
  109.0 1.2 copy-start.30
  170.0 69.6 %copy-start.1 = (f32[1,1,256,512]{3,2,1,0:T(8,128)}, f32[1,1,256,512]{3,2,1,0:T(8,128)S(1)}, u32[]{:S(2)}) copy-start(f32[1,1,256,512]{3,2,1,0:T(8,128)S(1)} %fusion.13) | copy-start | bytes 1572868
  176.3 63.4 %copy-start.2 = (f32[1,1,256,512]{3,2,1,0:T(8,128)}, f32[1,1,256,512]{3,2,1,0:T(8,128)S(1)}, u32[]{:S(2)}) copy-start(f32[1,1,256,512]{3,2,1,0:T(8,128)S(1)} %fusion.12) | copy-start | bytes 1572868
  176.8 4.0 collective-permute-start.2
  177.9 4.0 collective-permute-start.3
  181.8 1.2 copy-start.9
  183.4 16.3 %copy-start.22 = (f32[1,1,256,512]{3,2,1,0:T(8,128)}, f32[1,1,256,512]{3,2,1,0:T(8,128)S(1)}, u32[]{:S(2)}) copy-start(f32[1,1,256,512]{3,2,1,0:T(8,128)S(1)} %get-tuple-element.104) | copy-start | bytes 1572868
  183.4 16.3 %copy-start.23 = (f32[1,1,256,512]{3,2,1,0:T(8,128)}, f32[1,1,256,512]{3,2,1,0:T(8,128)S(1)}, u32[]{:S(2)}) copy-start(f32[1,1,256,512]{3,2,1,0:T(8,128)S(1)} %get-tuple-element.105) | copy-start | bytes 1572868
  183.7 16.0 %collective-permute-start.4 = (f32[2,1,256,512]{3,2,1,0:T(8,128)S(1)}, f32[2,1,256,512]{3,2,1,0:T(8,128)S(1)}, u32[]{:S(2)}, u32[]{:S(2)}) collective-permute-start(f32[2,1,256,512]{3,2,1,0:T(8,128)S(1)} %fusion.130), channel_id=1, source_target_pairs={{0,2},{2,4},{4,6},{6,8},{8,10},{10,12},{12,14},{14,16},{16,18},{18... | collective-permute-start | bytes 3145736 | tf_op jit(solution)/shard_map/ppermute | solution.py:42
  199.7 1.1 copy-start.26
  296.3 5.3 copy-start.48
  306.9 1.0 copy-start.37
  319.9 11.1 %copy-start.31 = (f32[2,4,64,512]{3,2,1,0:T(8,128)}, f32[2,4,64,512]{3,2,1,0:T(8,128)S(1)}, u32[]{:S(2)}) copy-start(f32[2,4,64,512]{3,2,1,0:T(8,128)S(1)} %maximum_multiply_fusion.5) | copy-start | bytes 3145732
  336.0 1.2 copy-start.32
  390.3 5.8 copy-start.49
  396.1 5.9 copy-start.40
  402.0 29.3 %copy-start.16 = (f32[1,1,256,512]{3,2,1,0:T(8,128)}, f32[1,1,256,512]{3,2,1,0:T(8,128)S(1)}, u32[]{:S(2)}) copy-start(f32[1,1,256,512]{3,2,1,0:T(8,128)S(1)} %fusion.9) | copy-start | bytes 1572868
  407.9 23.4 %copy-start.17 = (f32[1,1,256,512]{3,2,1,0:T(8,128)}, f32[1,1,256,512]{3,2,1,0:T(8,128)S(1)}, u32[]{:S(2)}) copy-start(f32[1,1,256,512]{3,2,1,0:T(8,128)S(1)} %fusion.8) | copy-start | bytes 1572868
  408.5 4.0 collective-permute-start.5
  409.5 4.0 collective-permute-start.6
  413.5 1.2 copy-start.10
  415.3 16.0 %collective-permute-start.7 = (f32[2,1,256,512]{3,2,1,0:T(8,128)S(1)}, f32[2,1,256,512]{3,2,1,0:T(8,128)S(1)}, u32[]{:S(2)}, u32[]{:S(2)}) collective-permute-start(f32[2,1,256,512]{3,2,1,0:T(8,128)S(1)} %fusion.128), channel_id=1, source_target_pairs={{0,2},{2,4},{4,6},{6,8},{8,10},{10,12},{12,14},{14,16},{16,18},{18... | collective-permute-start | bytes 3145736 | tf_op jit(solution)/shard_map/ppermute | solution.py:42
  532.7 6.1 copy-start.43
  532.7 6.1 copy-start.50
  544.1 1.0 copy-start.38
  557.3 10.9 %copy-start.33 = (f32[2,4,64,512]{3,2,1,0:T(8,128)}, f32[2,4,64,512]{3,2,1,0:T(8,128)S(1)}, u32[]{:S(2)}) copy-start(f32[2,4,64,512]{3,2,1,0:T(8,128)S(1)} %maximum_multiply_fusion.9) | copy-start | bytes 3145732
  576.0 2.3 copy-start.34
  586.9 1.4 copy-start.27
  637.2 6.7 copy-start.44
  637.2 6.7 copy-start.51
  644.0 6.3 copy-start.41
  650.2 29.3 %copy-start.18 = (f32[1,1,256,512]{3,2,1,0:T(8,128)}, f32[1,1,256,512]{3,2,1,0:T(8,128)S(1)}, u32[]{:S(2)}) copy-start(f32[1,1,256,512]{3,2,1,0:T(8,128)S(1)} %fusion.5) | copy-start | bytes 1572868
  656.1 23.5 %copy-start.19 = (f32[1,1,256,512]{3,2,1,0:T(8,128)}, f32[1,1,256,512]{3,2,1,0:T(8,128)S(1)}, u32[]{:S(2)}) copy-start(f32[1,1,256,512]{3,2,1,0:T(8,128)S(1)} %fusion.4) | copy-start | bytes 1572868
  656.7 4.0 collective-permute-start.8
  657.7 4.0 collective-permute-start.9
  661.7 1.2 copy-start.11
  663.5 16.0 %collective-permute-start.10 = (f32[2,1,256,512]{3,2,1,0:T(8,128)S(1)}, f32[2,1,256,512]{3,2,1,0:T(8,128)S(1)}, u32[]{:S(2)}, u32[]{:S(2)}) collective-permute-start(f32[2,1,256,512]{3,2,1,0:T(8,128)S(1)} %fusion.126), channel_id=1, source_target_pairs={{0,2},{2,4},{4,6},{6,8},{8,10},{10,12},{12,14},{14,16},{16,18},{18... | collective-permute-start | bytes 3145736 | tf_op jit(solution)/shard_map/ppermute | solution.py:42
  680.7 1.2 copy-start.14
  782.9 6.1 copy-start.45
  782.9 6.1 copy-start.52
  807.2 10.9 %copy-start.35 = (f32[2,4,64,512]{3,2,1,0:T(8,128)}, f32[2,4,64,512]{3,2,1,0:T(8,128)S(1)}, u32[]{:S(2)}) copy-start(f32[2,4,64,512]{3,2,1,0:T(8,128)S(1)} %maximum_multiply_fusion.13) | copy-start | bytes 3145732
  825.9 2.3 copy-start.36
  836.9 1.4 copy-start.28
  887.4 6.7 copy-start.46
  887.4 6.7 copy-start.53
  894.2 6.0 copy-start.42
  900.2 13.1 %copy-start.20 = (f32[1,1,256,512]{3,2,1,0:T(8,128)}, f32[1,1,256,512]{3,2,1,0:T(8,128)S(1)}, u32[]{:S(2)}) copy-start(f32[1,1,256,512]{3,2,1,0:T(8,128)S(1)} %fusion.1) | copy-start | bytes 1572868
  906.1 7.2 copy-start.21
  906.7 4.0 collective-permute-start.11
  907.7 4.0 collective-permute-start.12
  911.7 1.2 copy-start.12
  913.3 1.4 copy-start.24
  913.3 1.4 copy-start.25
  914.6 16.4 %collective-permute-start.13 = (f32[2,1,256,512]{3,2,1,0:T(8,128)}, f32[2,1,256,512]{3,2,1,0:T(8,128)}, u32[]{:S(2)}, u32[]{:S(2)}) collective-permute-start(f32[2,1,256,512]{3,2,1,0:T(8,128)} %fusion.124), channel_id=1, source_target_pairs={{0,2},{2,4},{4,6},{6,8},{8,10},{10,12},{12,14},{14,16},{16,18},{18... | collective-permute-start | bytes 3145736 | tf_op jit(solution)/shard_map/ppermute | solution.py:42
  919.9 14.0 %copy-start.13 = (f32[2,1,256,512]{3,2,1,0:T(8,128)S(1)}, f32[2,1,256,512]{3,2,1,0:T(8,128)}, u32[]{:S(2)}) copy-start(f32[2,1,256,512]{3,2,1,0:T(8,128)} %get-tuple-element.88) | copy-start | bytes 3145732
  933.9 1.2 copy-start.15
  (5 other events, 5.2 us)
where the time goes:
time: 1030 us; the launch traced here: 1020 us
  blocking collectives  401 us (39%)
  matrix products  389 us (38%)
  waiting for transfers between devices  72.3 us (7%)
  local copies, waits for them, and re-layouts  60.9 us (6%)
  starting transfers between devices  44.7 us (4%)
  other arithmetic  36.5 us (4%)
  between operations  13.1 us (1%)
    psum x25, blocking collectives, by_axis(): return functools.reduce(lax.psum, axes, value)  184 us
    all_to_all x8, blocking collectives, exchange_in_pieces(): lax.all_to_all(piece, axis, split_axis=0, concat_axis=0, tiled=True)  140 us
    dot_general x24, matrix products, mix(): jnp.einsum(pattern, field[0], sine, precision=highest)  102 us
    dot_general x24, matrix products, mix(): jnp.einsum(pattern, field[0], cosine, precision=highest)  96.7 us
    dot_general x24, matrix products, mix(): jnp.einsum(pattern, field[1], cosine, precision=highest)  95.7 us
    dot_general x24, matrix products, mix(): jnp.einsum(pattern, field[1], sine, precision=highest)  94.5 us
    all_to_all x3, blocking collectives, shards(): lax.all_to_all(flat, TM_SPACE, split_axis=1, concat_axis=2, tiled=True)  77 us
    ppermute x4, waiting for transfers between devices, shifted(): lax.ppermute(value, axis, [(source, source + steps) for source in range(l...  46.2 us
  transfers between devices with their start and end apart: 15, of which 13 were waited for; matrix products, arithmetic and copies ran while one was open for 0% of the time, Pallas kernels for 0%

commit v1 on v0

v1 whole, which is shorter than its diff:
```python
import math

import jax
import jax.numpy as jnp
import numpy as np
from jax import lax
from jax.experimental import pallas as pl
from jax.experimental.pallas import tpu as pltpu
from jax.sharding import Mesh
from jax.sharding import PartitionSpec as P

NX = 512
NY = 512
HALF = 256
TIME = 64
ITERS = 4
DEVICES = 128
TM = ("tm_0", "tm_1", "tm_2", "tm_3")
TM_SPACE = ("tm_0", "tm_1", "tm_2", "tm_3", "space")

tau = 400.0
alpha = 0.4
shift = alpha * alpha / (1.0 - alpha * alpha)
scale = alpha / (1.0 - alpha * alpha)
highest = lax.Precision.HIGHEST
f32 = jnp.float32
bf16 = jnp.bfloat16


def dft_tables():
    mode = np.arange(HALF)[:, None]
    cell = np.arange(HALF)[None, :]
    stack = []
    for frequency, transposed in ((2 * mode, False), (2 * mode + 1, False), (2 * mode + 1, True)):
        angle = 2.0 * np.pi * ((frequency * cell) % NX) / NX
        parts = [np.cos(angle), np.sin(angle)]
        stack.append(np.concatenate([part.T if transposed else part for part in parts]))
    exact = np.stack(stack)
    high = exact.astype(bf16)
    low = (exact - high.astype(np.float64)).astype(bf16)
    return np.stack([high, low])


TABLES = dft_tables()
EVEN, ODD, ODD_T = 0, 1, 2


def halves(value):
    high = value.astype(bf16)
    return high, (value - high.astype(f32)).astype(bf16)


def dot(left, right):
    return jnp.dot(left, right, preferred_element_type=f32)


def table_times(table, which, value):
    high, low = halves(value)
    return dot(table[0, which], high) + dot(table[1, which], high) + dot(table[0, which], low)


def times_table(value, table, which):
    high, low = halves(value)
    return dot(high, table[0, which]) + dot(high, table[1, which]) + dot(low, table[0, which])


def upper_rows(shape):
    return lax.broadcasted_iota(jnp.int32, shape, len(shape) - 2) < 4


def swapped(value):
    return pltpu.roll(value, 4, value.ndim - 2)


def signs(shape, upper, lower):
    return jnp.where(upper_rows(shape), f32(upper), f32(lower))


def split_parts(block):
    pair = block.reshape(32, 2, 8, HALF)
    first, second = pair[:, 0], pair[:, 1]
    upper = upper_rows((1, 8, 1))
    real = jnp.where(upper, first, swapped(second))
    imag = jnp.where(upper, swapped(first), second)
    return real.reshape(HALF, HALF), imag.reshape(HALF, HALF)


def merge_parts(real, imag):
    real = real.reshape(32, 8, HALF)
    imag = imag.reshape(32, 8, HALF)
    upper = upper_rows((1, 8, 1))
    first = jnp.where(upper, real, swapped(imag))
    second = jnp.where(upper, swapped(real), imag)
    return jnp.stack([first, second], axis=1).reshape(64, 8, HALF)


def cells_kernel(arrived, damping, table, field, sent):
    def inverse(part, which):
        real, imag = split_parts(arrived[pl.ds(part * 64, 64)])
        product = table_times(table, which, jnp.concatenate([real, imag], axis=1))
        top, bottom = product[:HALF], product[HALF:]
        return top[:, :HALF] - bottom[:, HALF:], top[:, HALF:] + bottom[:, :HALF]

    even_real, even_imag = inverse(0, EVEN)
    odd_real, odd_imag = inverse(1, ODD_T)
    near = (even_real + odd_real, even_imag + odd_imag)
    far = (even_real - odd_real, even_imag - odd_imag)
    damped = []
    for place, (real, imag) in enumerate((near, far)):
        rows = pl.ds(place * HALF, HALF)
        field[0, rows] = real
        field[1, rows] = imag
        absorb = damping[0, rows]
        phase = damping[1, rows]
        damped.append((absorb * real - phase * imag, absorb * imag + phase * real))

    def forward(part, which, sign):
        value = jnp.concatenate(
            [damped[0][0] + sign * damped[1][0], damped[0][1] + sign * damped[1][1]], axis=1
        )
        product = table_times(table, which, value)
        top, bottom = product[:HALF], product[HALF:]
        sent[pl.ds(part * 64, 64)] = merge_parts(
            top[:, :HALF] + bottom[:, HALF:], top[:, HALF:] - bottom[:, :HALF]
        )

    forward(0, EVEN, 1.0)
    forward(1, ODD, -1.0)


def on_cells(arrived, damping, table):
    return pl.pallas_call(
        cells_kernel,
        out_shape=(
            jax.ShapeDtypeStruct((2, NY, HALF), f32),
            jax.ShapeDtypeStruct((DEVICES, 8, HALF), f32),
        ),
        name="cells",
    )(arrived, damping, table)


def product_of(real, signed_imag, value):
    return real * value + signed_imag * swapped(value)


def rotation(angle_tangent):
    side = signs((8, NX), -1.0, 1.0)
    inverse = 1.0 / (1.0 + angle_tangent * angle_tangent)
    return (
        (1.0 - angle_tangent * angle_tangent) * inverse,
        -2.0 * angle_tangent * inverse * side,
        inverse,
        -angle_tangent * inverse * side,
    )


def multiplied(left, right):
    return left[0] * right[0] - left[1] * right[1], left[0] * right[1] + left[1] * right[0]


def wrap_factor(turn):
    side = signs((8, NX), -1.0, 1.0)
    power = turn
    for unused in range(6):
        power = multiplied(power, power)
        power = (power[0], power[1])
    return power, side


def rows_forward(block, count, table, into):
    pair = block.reshape(count, 2, 8, HALF)
    first, second = pair[:, 0], pair[:, 1]
    side = signs((1, 8, 1), 1.0, -1.0)
    for value, which, start in ((first + second, EVEN, 0), (first - second, ODD_T, HALF)):
        value = jnp.concatenate([value, side * swapped(value)], axis=2).reshape(8 * count, NX)
        into[:, :, pl.ds(start, HALF)] = times_table(value, table, which).reshape(count, 8, HALF)


def rows_inverse(modes, table, sent):
    side = signs((1, 8, 1), -1.0, 1.0)
    results = []
    for which, start in ((EVEN, 0), (ODD, HALF)):
        value = modes[:, :, pl.ds(start, HALF)]
        value = jnp.concatenate([value, side * swapped(value)], axis=2).reshape(TIME * 8, NX)
        results.append(times_table(value, table, which).reshape(TIME, 8, HALF))
    even, odd = results
    sent[...] = jnp.stack([even + odd, even - odd], axis=1).reshape(DEVICES, 8, HALF)


def signed_power(turn, count):
    side = signs((8, NX), -1.0, 1.0)
    real, imag = turn[0], turn[1] * side
    for unused in range(count):
        real, imag = real * real - imag * imag, 2.0 * real * imag
    return real, imag, side


def closing(turn):
    real, imag, side = signed_power(turn, 6)
    real, imag = alpha * real, alpha * imag
    rest = 1.0 - real
    inverse = 1.0 / (rest * rest + imag * imag)
    return (real * rest - imag * imag) * inverse, (imag * rest + real * imag) * inverse * side


def next_power(power, turn, conjugate):
    sign = -1.0 if conjugate else 1.0
    real = power[0] * turn[0] - sign * power[1] * turn[1]
    imag = sign * power[0] * turn[1] + power[1] * turn[0]
    return real, imag


NORMAL = 1.0 / (NX * NY)


def replay(turn, offset, summed, modes):
    def step(n, power):
        value = offset if summed is None else offset + summed[n]
        modes[n] = NORMAL * product_of(power[0], power[1], value)
        return next_power(power, turn, False)

    one = jnp.ones((8, NX), f32)
    lax.fori_loop(0, TIME, step, (one, jnp.zeros((8, NX), f32)), unroll=4)


def opening_kernel(block, tangent, table, vector, offset, sent, spectrum, modes):
    rows_forward(block[...], 2, table, spectrum)
    slope = tangent[...]
    turn_real, turn_imag, gain_real, gain_imag = rotation(slope)
    side = signs((8, NX), -1.0, 1.0)
    wave, damped = spectrum[0], spectrum[1]
    vector[...] = product_of(1.0, -slope * side, wave) - damped
    value = product_of(turn_real, turn_imag, wave) - product_of(gain_real, gain_imag, damped)
    wrap = product_of(*closing((turn_real, turn_imag)), value)
    offset[...] = wrap
    replay((turn_real, turn_imag), wrap + value, None, modes)
    rows_inverse(modes, table, sent)


def opening(block, tangent, table):
    return pl.pallas_call(
        opening_kernel,
        out_shape=(
            jax.ShapeDtypeStruct((8, NX), f32),
            jax.ShapeDtypeStruct((8, NX), f32),
            jax.ShapeDtypeStruct((DEVICES, 8, HALF), f32),
        ),
        scratch_shapes=[pltpu.VMEM((2, 8, NX), f32), pltpu.VMEM((TIME, 8, NX), f32)],
        name="opening",
    )(block, tangent, table)


def image_step(n, before, spectrum, slope_signed, offset, earlier):
    here = spectrum[n]
    value = here + before
    if earlier is not None:
        value = value - shift * earlier[n]
    return here, value * (1.0 / scale)


def wrapped_term(slope, offset):
    side = signs((8, NX), -1.0, 1.0)
    return offset + slope * side * swapped(offset)


def modes_kernel_of(first):
    def body(block, tangent, table, earlier, offset_in, vector, offset, sent, spectrum, summed):
        rows_forward(block[...], TIME, table, spectrum)
        slope = tangent[...]
        turn_real, turn_imag, gain_real, gain_imag = rotation(slope)
        turn = (turn_real, turn_imag)
        wrap = wrapped_term(slope, offset_in[...])
        if first:
            wrap = wrap - shift * earlier[...]

        def step(n, carry):
            before, total, power = carry
            here, value = image_step(n, before, spectrum, None, None, None if first else earlier)
            vector[n] = value
            total = total + product_of(power[0], power[1], value)
            summed[n] = total
            return here, total, next_power(power, turn, True)

        zero = jnp.zeros((8, NX), f32)
        unused, total, power = lax.fori_loop(
            0, TIME, step, (wrap, zero, (gain_real, gain_imag)), unroll=4
        )
        wrap = product_of(*closing(turn), total)
        offset[...] = wrap
        replay(turn, wrap, summed, spectrum)
        rows_inverse(spectrum, table, sent)

    return body


def on_modes(block, tangent, table, earlier, offset_in, first):
    return pl.pallas_call(
        modes_kernel_of(first),
        out_shape=(
            jax.ShapeDtypeStruct((TIME, 8, NX), f32),
            jax.ShapeDtypeStruct((8, NX), f32),
            jax.ShapeDtypeStruct((DEVICES, 8, HALF), f32),
        ),
        scratch_shapes=[pltpu.VMEM((TIME, 8, NX), f32), pltpu.VMEM((TIME, 8, NX), f32)],
        name="modes",
    )(block, tangent, table, earlier, offset_in)


PAIRS = [(i, j) for i in range(1, ITERS + 1) for j in range(i, ITERS + 1)]


def products_kernel(block, tangent, table, w0, w1, w2, w3, offset_in, totals, spectrum):
    rows_forward(block[...], TIME, table, spectrum)
    wrap = wrapped_term(tangent[...], offset_in[...])

    def narrowed(value):
        return value[:, 0:128] + value[:, 128:256] + value[:, 256:384] + value[:, 384:512]

    def step(n, carry):
        before, sums = carry
        here, value = image_step(n, before, spectrum, None, None, w3)
        vectors = (None, w1[n], w2[n], w3[n], value)
        sums = tuple(
            total + narrowed(vectors[i] * vectors[j]) for total, (i, j) in zip(sums, PAIRS)
        )
        return here, sums

    zero = jnp.zeros((8, 128), f32)
    start = w0[...]
    here, first = image_step(0, wrap, spectrum, None, None, w3)
    heads = (start, w1[0], w2[0], w3[0], first)
    for i, vector in enumerate(heads):
        totals[i] = narrowed(start * vector)
    sums = tuple(narrowed(heads[i] * heads[j]) for i, j in PAIRS)
    unused, sums = lax.fori_loop(1, TIME, step, (here, sums), unroll=3)
    for place, total in enumerate(sums):
        totals[place + 5] = total
    totals[15] = zero


def products(block, tangent, table, vectors, offset_in):
    return pl.pallas_call(
        products_kernel,
        out_shape=jax.ShapeDtypeStruct((16, 8, 128), f32),
        scratch_shapes=[pltpu.VMEM((TIME, 8, NX), f32)],
        name="products",
    )(block, tangent, table, *vectors, offset_in)


def least_squares(gram):
    size = ITERS + 1
    root = [[None] * size for unused in range(size)]
    for i in range(size):
        for j in range(i, size):
            total = gram[i][j]
            for k in range(i):
                total = total - root[k][i] * root[k][j]
            root[i][j] = jnp.sqrt(total) if i == j else total / root[i][i]
    matrix = [[jnp.zeros_like(gram[0][0]) for unused in range(ITERS)] for other in range(size)]
    for column in range(ITERS):
        for row in range(column + 2):
            total = scale * root[row][column + 1]
            if row <= column:
                total = total + (1.0 + shift) * root[row][column]
            matrix[row][column] = total
    target = [root[0][0]] + [jnp.zeros_like(gram[0][0]) for unused in range(ITERS)]
    cosines = []
    sines = []
    for column in range(ITERS):
        for row in range(column):
            upper = matrix[row][column]
            lower = matrix[row + 1][column]
            matrix[row][column] = cosines[row] * upper + sines[row] * lower
            matrix[row + 1][column] = -sines[row] * upper + cosines[row] * lower
        upper = matrix[column][column]
        lower = matrix[column + 1][column]
        radius = jnp.sqrt(upper * upper + lower * lower)
        cosines.append(upper / radius)
        sines.append(lower / radius)
        matrix[column][column] = radius
        target[column + 1] = -sines[column] * target[column]
        target[column] = cosines[column] * target[column]
    factors = [None] * ITERS
    for row in reversed(range(ITERS)):
        total = target[row]
        for other in range(row + 1, ITERS):
            total = total - matrix[row][other] * factors[other]
        factors[row] = total / matrix[row][row]
    return factors


def combine_kernel(totals, z0, z1, z2, z3, out):
    summed = jnp.sum(totals[...], axis=0)
    size = ITERS + 1
    gram = [[None] * size for unused in range(size)]
    order = [(0, j) for j in range(size)] + PAIRS
    for place, (i, j) in enumerate(order):
        value = jnp.sum(summed[place : place + 1, :], axis=1, keepdims=True)
        gram[i][j] = value
        gram[j][i] = value
    factors = least_squares(gram)
    for part in range(2):
        value = factors[0] * z0[part]
        for factor, other in zip(factors[1:], (z1, z2, z3)):
            value = value + factor * other[part]
        out[part, 0] = value.T


def combine(totals, fields):
    return pl.pallas_call(
        combine_kernel,
        out_shape=jax.ShapeDtypeStruct((2, 1, HALF, NY), f32),
        name="combine",
    )(totals, *fields)


def exchange(value):
    return lax.all_to_all(value, TM_SPACE, split_axis=0, concat_axis=0, tiled=True)


def column_modes(first, count):
    order = first + jnp.arange(count, dtype=jnp.int32)
    return 2 * (order % HALF) + order // HALF


def shards(u_init, phase, absorb):
    step = lax.axis_index(TM)
    half = lax.axis_index("space")
    table = jnp.asarray(TABLES)
    damping = 0.5 * jnp.stack([absorb, phase])
    modes = column_modes(8 * step, 8)
    turns = modes[:, None] * jnp.arange(NY, dtype=jnp.int32)[None, :] % NY
    angle = turns.astype(f32) * (2.0 * math.pi / NY)
    damped = jnp.stack(
        [
            damping[0] * u_init[0] - damping[1] * u_init[1],
            damping[0] * u_init[1] + damping[1] * u_init[0],
        ]
    )
    fields = jnp.stack([u_init, damped])
    cosine = jnp.einsum("fcxy,ky->fckx", fields, jnp.cos(angle), precision=highest)
    sine = jnp.einsum("fcxy,ky->fckx", fields, jnp.sin(angle), precision=highest)
    columns = jnp.stack([cosine[:, 0] + sine[:, 1], cosine[:, 1] - sine[:, 0]], axis=1)
    columns = columns.reshape(2, 2, 2, 4, HALF)
    mine = lax.dynamic_index_in_dim(columns, half, 2, keepdims=False).reshape(2, 8, HALF)
    theirs = lax.dynamic_index_in_dim(columns, 1 - half, 2, keepdims=False).reshape(2, 8, HALF)
    theirs = lax.ppermute(theirs, "space", [(0, 1), (1, 0)])
    block = jnp.where(
        half == 0, jnp.stack([mine, theirs], axis=1), jnp.stack([theirs, mine], axis=1)
    ).reshape(4, 8, HALF)
    own = column_modes(8 * step + 4 * half, 4).astype(f32)
    rows = jnp.arange(HALF, dtype=jnp.int32)
    rows = jnp.concatenate([2 * rows, 2 * rows + 1]).astype(f32)
    symbol_y = 4.0 * jnp.sin(own * (math.pi / NY)) ** 2
    symbol_x = 4.0 * jnp.sin(rows * (math.pi / NX)) ** 2
    tangent = (0.5 * tau) * (jnp.concatenate([symbol_y, symbol_y])[:, None] + symbol_x[None, :])
    damping = damping.swapaxes(1, 2)

    vector, offset, sent = opening(block, tangent, table)
    vectors = [vector]
    found = []
    for column in range(ITERS):
        field, sent = on_cells(exchange(sent), damping, table)
        found.append(field)
        arrived = exchange(sent)
        if column + 1 < ITERS:
            vector, offset, sent = on_modes(
                arrived, tangent, table, vectors[-1], offset, column == 0
            )
            vectors.append(vector)
    totals = products(arrived, tangent, table, vectors, offset)
    totals = jnp.sum(totals, axis=1)
    spread = jnp.broadcast_to(totals[None], (DEVICES, 16, 128))
    return combine(exchange(spread), found)


def solution(mesh):
    torus = Mesh(
        mesh.devices.reshape(4, 4, 2, 2, mesh.shape["space"]),
        ("tm_0", "tm_1", "tm_2", "tm_3", "space"),
    )
    placed = (P(None, "space", None), P("space", None), P("space", None))
    return jax.shard_map(
        shards, mesh=torus, in_specs=placed, out_specs=P(None, TM, "space", None), check_vma=False
    )
```

time: 1030 us -> 290 us (0.28); the launches traced: 1020 us -> 289 us
  matrix products: 389 us -> 2.44 us
  blocking collectives: 401 us -> 224 us
  waiting for transfers between devices: 72.3 us -> 0.25 us
  local copies, waits for them, and re-layouts: 60.9 us -> 3.04 us
  Pallas kernels: 0 us -> 52.5 us
  starting transfers between devices: 44.7 us -> 3.64 us
  other arithmetic: 36.5 us -> 3.7 us
  between operations: 13.1 us -> 0.13 us
    dot_general x96 -> x2, matrix products: 389 us -> 2.44 us  [the longest x1 1.22 us: shards(): jnp.einsum('fcxy,ky->fckx', fields, jnp.cos(angle), precision=highest)]
    psum x25 -> x0, blocking collectives: 184 us -> none  [by_axis(): return functools.reduce(lax.psum, axes, value)]
    ppermute x14 -> x1, waiting for transfers between devices: 53.6 us -> 0.25 us  [shards(): theirs = lax.ppermute(theirs, 'space', [(0, 1), (1, 0)])]
    pallas_call x0 -> x10, Pallas kernels: none -> 52.5 us  [the longest x4 20.8 us: on_cells(): pl.pallas_call(cells_kernel, out_shape=(jax.ShapeDtypeStruct((2, NY, HALF...]
    ppermute x14 -> x1, starting transfers between devices: 33.1 us -> 3.64 us  [shards(): theirs = lax.ppermute(theirs, 'space', [(0, 1), (1, 0)])]
    another operation x24 -> x4, local copies, waits for them, and re-layouts: 27.5 us -> 0.04 us  [the longest x3 0.03 us: shards(): jnp.stack([cosine[:, 0] + sine[:, 1], cosine[:, 1] - sine[:, 0]], axis=1)]
    all_to_all x1 -> x0, waiting for transfers between devices: 18.8 us -> none  [shards(): lax.all_to_all(flat, TM_SPACE, split_axis=1, concat_axis=2, tiled=True)]
    reduce_sum x8 -> x1, other arithmetic: 13.6 us -> 0.86 us  [shards(): totals = jnp.sum(totals, axis=1)]
  transfers between devices with their start and end apart: 15 -> 1, of which waited for: 13 -> 1; matrix products, arithmetic and copies ran while one was open for 0% -> 0% of each run, Pallas kernels for 0% -> 0%
where the time goes in v1:
time: 290 us; the launch traced here: 289 us
  blocking collectives  224 us (77%)
  Pallas kernels  52.5 us (18%)
  other arithmetic  3.7 us (1%)
  starting transfers between devices  3.64 us (1%)
  local copies, waits for them, and re-layouts  3.04 us (1%)
    all_to_all x9, blocking collectives, exchange(): lax.all_to_all(value, TM_SPACE, split_axis=0, concat_axis=0, tiled=True)  224 us
    pallas_call x4, Pallas kernels, on_cells(): pl.pallas_call(cells_kernel, out_shape=(jax.ShapeDtypeStruct((2, NY, HALF...  20.8 us
    pallas_call x3, Pallas kernels, on_modes(): pl.pallas_call(modes_kernel_of(first), out_shape=(jax.ShapeDtypeStruct((T...  18.3 us
  transfers between devices with their start and end apart: 1, of which 1 were waited for; matrix products, arithmetic and copies ran while one was open for 0% of the time, Pallas kernels for 0%

profile of v1, /device:TPU:1, one launch (start us, length us, event | category | flops | bytes accessed | tf_op | source)
XLA Modules:
  0.0 289.4 jit_solution(7994468210858284460)
XLA Ops:
  0.0 0.0 copy-start
  0.0 1.3 copy.7
  1.3 1.2 copy.6
  2.6 0.0 copy-done
  2.6 0.3 copy.5
  2.9 1.1 fusion.34
  4.1 0.1 multiply_subtract_fusion
  4.2 0.1 maximum_bitcast_fusion
  4.3 1.2 fusion.3
  5.5 1.2 fusion.2
  6.9 3.6 %collective-permute-start = (f32[2,8,256]{2,1,0:T(8,128)S(1)}, f32[2,8,256]{2,1,0:T(8,128)S(1)}, u32[]{:S(2)}, u32[]{:S(2)}) collective-permute-start(f32[2,8,256]{2,1,0:T(8,128)S(1)} %reshape.64), channel_id=1, source_target_pairs={{0,1},{1,0},{2,3},{3,2},{4,5},{5,4},{6,7},{7,6},{8,9},{9,8},{10,11... | collective-permute-start | bytes 49160 | tf_op jit(solution)/shard_map/ppermute | solution.py:447
  10.5 0.1 multiply_multiply_fusion
  10.6 0.1 pad_maximum_fusion.7
  10.7 0.7 add_multiply_fusion.tangent
  11.4 0.2 collective-permute-done
  11.6 0.6 maximum_select_fusion
  12.2 4.1 %opening.1 = (f32[8,512]{1,0:T(8,128)}, f32[8,512]{1,0:T(8,128)}, f32[128,8,256]{2,1,0:T(8,128)}) custom-call(f32[4,8,256]{2,1,0:T(8,128)} %bitcast.35, f32[8,512]{1,0:T(8,128)} %add_multiply_fusion.tangent, bf16[2,3,512,256]{3,2,1,0:T(8,128)(2,1)} %constant.114.clone.table), custom_call_target="tpu_custom_call" | custom-call | tf_op jit(solution)/shard_map/opening/pallas_call | solution.py:241
  16.4 31.3 %all_to_all.45.arrived = f32[128,8,256]{2,1,0:T(8,128)} all-to-all(f32[128,8,256]{2,1,0:T(8,128)} %get-tuple-element.25), channel_id=1, replica_groups=mesh['tm_0'=4,'tm_1'=4,'tm_2'=2,'tm_3'=2,'space'=2] {'tm_0','tm_1','tm_2..., dimensions={0} | all-to-all | bytes 2097152 | tf_op jit(solution)/shard_map/all_to_all | solution.py:418
  47.7 5.2 %cells.4 = (f32[2,512,256]{2,1,0:T(8,128)}, f32[128,8,256]{2,1,0:T(8,128)}) custom-call(f32[128,8,256]{2,1,0:T(8,128)} %all_to_all.45.arrived, f32[2,512,256]{2,1,0:T(8,128)} %get-tuple-element.47.damping, bf16[2,3,512,256]{3,2,1,0:T(8,128)(2,1)} %constant.114.clone.table), custom_call_target="tpu_custom_call" | custom-call | tf_op jit(solution)/shard_map/cells/pallas_call | solution.py:132
  52.9 24.1 %all_to_all.46.block = f32[128,8,256]{2,1,0:T(8,128)} all-to-all(f32[128,8,256]{2,1,0:T(8,128)} %get-tuple-element.26), channel_id=1, replica_groups=mesh['tm_0'=4,'tm_1'=4,'tm_2'=2,'tm_3'=2,'space'=2] {'tm_0','tm_1','tm_2..., dimensions={0} | all-to-all | bytes 2097152 | tf_op jit(solution)/shard_map/all_to_all | solution.py:418
  77.0 5.8 %modes.3 = (f32[64,8,512]{2,1,0:T(8,128)}, f32[8,512]{1,0:T(8,128)}, f32[128,8,256]{2,1,0:T(8,128)}) custom-call(f32[128,8,256]{2,1,0:T(8,128)} %all_to_all.46.block, f32[8,512]{1,0:T(8,128)} %add_multiply_fusion.tangent, bf16[2,3,512,256]{3,2,1,0:T(8,128)(2,1)} %constant.114.clone.table, f32[8,512]{1,0:T(8,128)} %get-tuple-element.27.earlier.w0, ...), custom_call_target="tpu_custom_call" | custom-call | tf_op jit(solution)/shard_map/modes/pallas_call | solution.py:297
  82.8 24.1 %all_to_all.47.arrived = f32[128,8,256]{2,1,0:T(8,128)} all-to-all(f32[128,8,256]{2,1,0:T(8,128)} %get-tuple-element.29), channel_id=1, replica_groups=mesh['tm_0'=4,'tm_1'=4,'tm_2'=2,'tm_3'=2,'space'=2] {'tm_0','tm_1','tm_2..., dimensions={0} | all-to-all | bytes 2097152 | tf_op jit(solution)/shard_map/all_to_all | solution.py:418
  106.9 5.2 %cells.5 = (f32[2,512,256]{2,1,0:T(8,128)}, f32[128,8,256]{2,1,0:T(8,128)}) custom-call(f32[128,8,256]{2,1,0:T(8,128)} %all_to_all.47.arrived, f32[2,512,256]{2,1,0:T(8,128)} %get-tuple-element.47.damping, bf16[2,3,512,256]{3,2,1,0:T(8,128)(2,1)} %constant.114.clone.table), custom_call_target="tpu_custom_call" | custom-call | tf_op jit(solution)/shard_map/cells/pallas_call | solution.py:132
  112.1 24.1 %all_to_all.48.block = f32[128,8,256]{2,1,0:T(8,128)} all-to-all(f32[128,8,256]{2,1,0:T(8,128)} %get-tuple-element.30), channel_id=1, replica_groups=mesh['tm_0'=4,'tm_1'=4,'tm_2'=2,'tm_3'=2,'space'=2] {'tm_0','tm_1','tm_2..., dimensions={0} | all-to-all | bytes 2097152 | tf_op jit(solution)/shard_map/all_to_all | solution.py:418
  136.2 6.2 %modes.4 = (f32[64,8,512]{2,1,0:T(8,128)}, f32[8,512]{1,0:T(8,128)}, f32[128,8,256]{2,1,0:T(8,128)}) custom-call(f32[128,8,256]{2,1,0:T(8,128)} %all_to_all.48.block, f32[8,512]{1,0:T(8,128)} %add_multiply_fusion.tangent, bf16[2,3,512,256]{3,2,1,0:T(8,128)(2,1)} %constant.114.clone.table, f32[64,8,512]{2,1,0:T(8,128)} %get-tuple-element.31.earlier.w1, ...), custom_call_target="tpu_custom_call" | custom-call | tf_op jit(solution)/shard_map/modes/pallas_call | solution.py:297
  142.5 24.1 %all_to_all.49.arrived = f32[128,8,256]{2,1,0:T(8,128)} all-to-all(f32[128,8,256]{2,1,0:T(8,128)} %get-tuple-element.33), channel_id=1, replica_groups=mesh['tm_0'=4,'tm_1'=4,'tm_2'=2,'tm_3'=2,'space'=2] {'tm_0','tm_1','tm_2..., dimensions={0} | all-to-all | bytes 2097152 | tf_op jit(solution)/shard_map/all_to_all | solution.py:418
  166.6 5.2 %cells.6 = (f32[2,512,256]{2,1,0:T(8,128)}, f32[128,8,256]{2,1,0:T(8,128)}) custom-call(f32[128,8,256]{2,1,0:T(8,128)} %all_to_all.49.arrived, f32[2,512,256]{2,1,0:T(8,128)} %get-tuple-element.47.damping, bf16[2,3,512,256]{3,2,1,0:T(8,128)(2,1)} %constant.114.clone.table), custom_call_target="tpu_custom_call" | custom-call | tf_op jit(solution)/shard_map/cells/pallas_call | solution.py:132
  171.8 24.1 %all_to_all.50.block = f32[128,8,256]{2,1,0:T(8,128)} all-to-all(f32[128,8,256]{2,1,0:T(8,128)} %get-tuple-element.34), channel_id=1, replica_groups=mesh['tm_0'=4,'tm_1'=4,'tm_2'=2,'tm_3'=2,'space'=2] {'tm_0','tm_1','tm_2..., dimensions={0} | all-to-all | bytes 2097152 | tf_op jit(solution)/shard_map/all_to_all | solution.py:418
  195.9 6.3 %modes.5 = (f32[64,8,512]{2,1,0:T(8,128)}, f32[8,512]{1,0:T(8,128)}, f32[128,8,256]{2,1,0:T(8,128)}) custom-call(f32[128,8,256]{2,1,0:T(8,128)} %all_to_all.50.block, f32[8,512]{1,0:T(8,128)} %add_multiply_fusion.tangent, bf16[2,3,512,256]{3,2,1,0:T(8,128)(2,1)} %constant.114.clone.table, f32[64,8,512]{2,1,0:T(8,128)} %get-tuple-element.35.earlier.w2, ...), custom_call_target="tpu_custom_call" | custom-call | tf_op jit(solution)/shard_map/modes/pallas_call | solution.py:297
  202.2 24.1 %all_to_all.51.arrived = f32[128,8,256]{2,1,0:T(8,128)} all-to-all(f32[128,8,256]{2,1,0:T(8,128)} %get-tuple-element.37), channel_id=1, replica_groups=mesh['tm_0'=4,'tm_1'=4,'tm_2'=2,'tm_3'=2,'space'=2] {'tm_0','tm_1','tm_2..., dimensions={0} | all-to-all | bytes 2097152 | tf_op jit(solution)/shard_map/all_to_all | solution.py:418
  226.3 5.2 %cells.7 = (f32[2,512,256]{2,1,0:T(8,128)}, f32[128,8,256]{2,1,0:T(8,128)}) custom-call(f32[128,8,256]{2,1,0:T(8,128)} %all_to_all.51.arrived, f32[2,512,256]{2,1,0:T(8,128)} %get-tuple-element.47.damping, bf16[2,3,512,256]{3,2,1,0:T(8,128)(2,1)} %constant.114.clone.table), custom_call_target="tpu_custom_call" | custom-call | tf_op jit(solution)/shard_map/cells/pallas_call | solution.py:132
  231.5 24.4 %all_to_all.52.block = f32[128,8,256]{2,1,0:T(8,128)} all-to-all(f32[128,8,256]{2,1,0:T(8,128)} %get-tuple-element.38), channel_id=1, replica_groups=mesh['tm_0'=4,'tm_1'=4,'tm_2'=2,'tm_3'=2,'space'=2] {'tm_0','tm_1','tm_2..., dimensions={0} | all-to-all | bytes 2097152 | tf_op jit(solution)/shard_map/all_to_all | solution.py:418
  255.9 5.2 %products.1 = f32[16,8,128]{2,1,0:T(8,128)} custom-call(f32[128,8,256]{2,1,0:T(8,128)} %all_to_all.52.block, f32[8,512]{1,0:T(8,128)} %add_multiply_fusion.tangent, bf16[2,3,512,256]{3,2,1,0:T(8,128)(2,1)} %constant.114.clone.table, f32[8,512]{1,0:T(8,128)} %get-tuple-element.27.earlier.w0, f32[64,8,512]{2,1,0:T(8,128)} %get-tuple-element.31.earlier.w1, ...), custom_call_target="tpu_custom_call" | custom-call | tf_op jit(solution)/shard_map/products/pallas_call | solution.py:342
  261.1 0.9 reduce_sum.9
  261.9 0.1 broadcast_in_dim.2
  262.0 23.2 %all_to_all.53.totals = f32[128,16,128]{2,1,0:T(8,128)} all-to-all(f32[128,16,128]{2,1,0:T(8,128)S(1)} %broadcast_in_dim.2), channel_id=1, replica_groups=mesh['tm_0'=4,'tm_1'=4,'tm_2'=2,'tm_3'=2,'space'=2] {'tm_0','tm_1','tm_2..., dimensions={0} | all-to-all | bytes 2097152 | tf_op jit(solution)/shard_map/all_to_all | solution.py:418
  285.3 4.2 %combine.1 = f32[2,1,256,512]{3,2,1,0:T(8,128)} custom-call(f32[128,16,128]{2,1,0:T(8,128)} %all_to_all.53.totals, f32[2,512,256]{2,1,0:T(8,128)} %get-tuple-element.41.z0, f32[2,512,256]{2,1,0:T(8,128)} %get-tuple-element.42.z1, f32[2,512,256]{2,1,0:T(8,128)} %get-tuple-element.43.z2, f32[2,512,256]{2,1,0:T(8,128)} %get-tuple-element.44.z3), custom_call_target="tpu_custom_call" | custom-call | tf_op jit(solution)/shard_map/combine/pallas_call | solution.py:410
  (13 shorter events, 0.2 us)
Async XLA Ops:
  0.0 2.6 copy-start
  6.9 4.8 %collective-permute-start = (f32[2,8,256]{2,1,0:T(8,128)S(1)}, f32[2,8,256]{2,1,0:T(8,128)S(1)}, u32[]{:S(2)}, u32[]{:S(2)}) collective-permute-start(f32[2,8,256]{2,1,0:T(8,128)S(1)} %reshape.64), channel_id=1, source_target_pairs={{0,1},{1,0},{2,3},{3,2},{4,5},{5,4},{6,7},{7,6},{8,9},{9,8},{10,11... | collective-permute-start | bytes 49160 | tf_op jit(solution)/shard_map/ppermute | solution.py:447

commit v2 on v1

--- a/solution.py
+++ b/solution.py
@@ -64,6 +64,23 @@
     return dot(high, table[0, which]) + dot(high, table[1, which]) + dot(low, table[0, which])
 
 
+def call(body, out_shape, name, scratch, *operands):
+    inside = pl.BlockSpec(memory_space=pltpu.VMEM)
+    return pl.pallas_call(
+        body,
+        out_shape=out_shape,
+        in_specs=[inside] * len(operands),
+        out_specs=jax.tree.map(lambda unused: inside, out_shape),
+        scratch_shapes=scratch,
+        compiler_params=pltpu.CompilerParams(vmem_limit_bytes=24 << 20),
+        name=name,
+    )(*operands)
+
+
+def array(*shape):
+    return jax.ShapeDtypeStruct(shape, f32)
+
+
 def upper_rows(shape):
     return lax.broadcasted_iota(jnp.int32, shape, len(shape) - 2) < 4
 
@@ -129,14 +146,8 @@
 
 
 def on_cells(arrived, damping, table):
-    return pl.pallas_call(
-        cells_kernel,
-        out_shape=(
-            jax.ShapeDtypeStruct((2, NY, HALF), f32),
-            jax.ShapeDtypeStruct((DEVICES, 8, HALF), f32),
-        ),
-        name="cells",
-    )(arrived, damping, table)
+    shapes = (array(2, NY, HALF), array(DEVICES, 8, HALF))
+    return call(cells_kernel, shapes, "cells", (), arrived, damping, table)
 
 
 def product_of(real, signed_imag, value):
@@ -238,16 +249,9 @@
 
 
 def opening(block, tangent, table):
-    return pl.pallas_call(
-        opening_kernel,
-        out_shape=(
-            jax.ShapeDtypeStruct((8, NX), f32),
-            jax.ShapeDtypeStruct((8, NX), f32),
-            jax.ShapeDtypeStruct((DEVICES, 8, HALF), f32),
-        ),
-        scratch_shapes=[pltpu.VMEM((2, 8, NX), f32), pltpu.VMEM((TIME, 8, NX), f32)],
-        name="opening",
-    )(block, tangent, table)
+    shapes = (array(8, NX), array(8, NX), array(DEVICES, 8, HALF))
+    scratch = (pltpu.VMEM((2, 8, NX), f32), pltpu.VMEM((TIME, 8, NX), f32))
+    return call(opening_kernel, shapes, "opening", scratch, block, tangent, table)
 
 
 def image_step(n, before, spectrum, slope_signed, offset, earlier):
@@ -294,16 +298,10 @@
 
 
 def on_modes(block, tangent, table, earlier, offset_in, first):
-    return pl.pallas_call(
-        modes_kernel_of(first),
-        out_shape=(
-            jax.ShapeDtypeStruct((TIME, 8, NX), f32),
-            jax.ShapeDtypeStruct((8, NX), f32),
-            jax.ShapeDtypeStruct((DEVICES, 8, HALF), f32),
-        ),
-        scratch_shapes=[pltpu.VMEM((TIME, 8, NX), f32), pltpu.VMEM((TIME, 8, NX), f32)],
-        name="modes",
-    )(block, tangent, table, earlier, offset_in)
+    shapes = (array(TIME, 8, NX), array(8, NX), array(DEVICES, 8, HALF))
+    scratch = (pltpu.VMEM((TIME, 8, NX), f32), pltpu.VMEM((TIME, 8, NX), f32))
+    body = modes_kernel_of(first)
+    return call(body, shapes, "modes", scratch, block, tangent, table, earlier, offset_in)
 
 
 PAIRS = [(i, j) for i in range(1, ITERS + 1) for j in range(i, ITERS + 1)]
@@ -325,26 +323,24 @@
         )
         return here, sums
 
-    zero = jnp.zeros((8, 128), f32)
     start = w0[...]
     here, first = image_step(0, wrap, spectrum, None, None, w3)
     heads = (start, w1[0], w2[0], w3[0], first)
-    for i, vector in enumerate(heads):
-        totals[i] = narrowed(start * vector)
     sums = tuple(narrowed(heads[i] * heads[j]) for i, j in PAIRS)
     unused, sums = lax.fori_loop(1, TIME, step, (here, sums), unroll=3)
+    sums = tuple(narrowed(start * vector) for vector in heads) + sums
+    lane = lax.broadcasted_iota(jnp.int32, (1, 128), 1)
+    packed = jnp.zeros((1, 128), f32)
     for place, total in enumerate(sums):
-        totals[place + 5] = total
-    totals[15] = zero
+        total = jnp.sum(jnp.sum(total, axis=0, keepdims=True), axis=1, keepdims=True)
+        packed = jnp.where(lane == place, total, packed)
+    totals[...] = packed
 
 
 def products(block, tangent, table, vectors, offset_in):
-    return pl.pallas_call(
-        products_kernel,
-        out_shape=jax.ShapeDtypeStruct((16, 8, 128), f32),
-        scratch_shapes=[pltpu.VMEM((TIME, 8, NX), f32)],
-        name="products",
-    )(block, tangent, table, *vectors, offset_in)
+    scratch = (pltpu.VMEM((TIME, 8, NX), f32),)
+    operands = (block, tangent, table, *vectors, offset_in)
+    return call(products_kernel, array(1, 128), "products", scratch, *operands)
 
 
 def least_squares(gram):
@@ -390,12 +386,13 @@
 
 
 def combine_kernel(totals, z0, z1, z2, z3, out):
-    summed = jnp.sum(totals[...], axis=0)
+    summed = jnp.sum(totals[...], axis=0, keepdims=True)
     size = ITERS + 1
     gram = [[None] * size for unused in range(size)]
+    lane = lax.broadcasted_iota(jnp.int32, (1, 128), 1)
     order = [(0, j) for j in range(size)] + PAIRS
     for place, (i, j) in enumerate(order):
-        value = jnp.sum(summed[place : place + 1, :], axis=1, keepdims=True)
+        value = jnp.sum(jnp.where(lane == place, summed, 0.0), axis=1, keepdims=True)
         gram[i][j] = value
         gram[j][i] = value
     factors = least_squares(gram)
@@ -407,11 +404,7 @@
 
 
 def combine(totals, fields):
-    return pl.pallas_call(
-        combine_kernel,
-        out_shape=jax.ShapeDtypeStruct((2, 1, HALF, NY), f32),
-        name="combine",
-    )(totals, *fields)
+    return call(combine_kernel, array(2, 1, HALF, NY), "combine", (), totals, *fields)
 
 
 def exchange(value):
@@ -469,9 +462,7 @@
             )
             vectors.append(vector)
     totals = products(arrived, tangent, table, vectors, offset)
-    totals = jnp.sum(totals, axis=1)
-    spread = jnp.broadcast_to(totals[None], (DEVICES, 16, 128))
-    return combine(exchange(spread), found)
+    return combine(exchange(jnp.broadcast_to(totals, (DEVICES, 128))), found)
 
 
 def solution(mesh):

time: 290 us -> 241 us (0.83)
  Pallas kernels: 52.5 us -> 23.1 us
  blocking collectives: 224 us -> 205 us
  other arithmetic: 3.7 us -> 0.66 us
    pallas_call x10, Pallas kernels: 52.5 us -> 23.1 us  [call(): pl.pallas_call(body, out_shape=out_shape, in_specs=[inside] * len(operand...]
    all_to_all x9, blocking collectives: 224 us -> 205 us  [exchange(): lax.all_to_all(value, TM_SPACE, split_axis=0, concat_axis=0, tiled=True)]
where the time goes in v2:
time: 241 us
  blocking collectives  205 us (85%)
  Pallas kernels  23.1 us (10%)
  matrix products  3.78 us (2%)
  starting transfers between devices  3.64 us (2%)
  local copies, waits for them, and re-layouts  3.58 us (1%)
    all_to_all x9, blocking collectives, exchange(): lax.all_to_all(value, TM_SPACE, split_axis=0, concat_axis=0, tiled=True)  205 us
    pallas_call x10, Pallas kernels, call(): pl.pallas_call(body, out_shape=out_shape, in_specs=[inside] * len(operand...  23.1 us
  transfers between devices with their start and end apart: 1, of which 1 were waited for; matrix products, arithmetic and copies ran while one was open for 0% of the time, Pallas kernels for 0%

profile of v2, /device:TPU:1, one launch (start us, length us, event | category | flops | bytes accessed | tf_op | source)
XLA Modules:
  0.0 240.8 jit_solution(17112025154002533891)
XLA Ops:
  0.0 0.0 copy-start.2
  0.0 1.3 copy.16
  1.3 1.2 copy.15
  2.6 0.0 copy-done.2
  2.6 0.3 copy.14
  2.9 0.0 copy-start.1
  3.0 0.2 fusion.34
  3.1 0.1 multiply_subtract_fusion
  3.3 0.1 maximum_bitcast_fusion
  3.4 0.6 copy-done.1
  3.9 1.2 fusion.3
  5.1 0.0 copy-start
  5.1 2.6 %fusion.2 = f32[2,2,8,256]{3,2,1,0:T(8,128)S(1)} fusion(f32[1,2,256,512]{2,3,1,0:T(8,128)S(1)} %maximum_bitcast_fusion, f32[1,2,256,512]{2,3,1,0:T(8,128)} %bitcast.37, s32[8]{0:T(128)S(1)} %fusion.21), kind=kOutput, calls=%fused_computation.3 | convolution fusion | flops 50913280 | bytes 2129952 | tf_op jit(solution)/shard_map/fcxy,ky->fckx/dot_general | solution.py:434
  7.8 3.6 %collective-permute-start = (f32[2,8,256]{2,1,0:T(8,128)S(1)}, f32[2,8,256]{2,1,0:T(8,128)S(1)}, u32[]{:S(2)}, u32[]{:S(2)}) collective-permute-start(f32[2,8,256]{2,1,0:T(8,128)S(1)} %reshape.69), channel_id=1, source_target_pairs={{0,1},{1,0},{2,3},{3,2},{4,5},{5,4},{6,7},{7,6},{8,9},{9,8},{10,11... | collective-permute-start | bytes 49160 | tf_op jit(solution)/shard_map/ppermute | solution.py:440
  11.5 0.1 multiply_multiply_fusion
  11.5 0.1 pad_maximum_fusion.7
  11.6 0.1 add_multiply_fusion.tangent
  11.7 0.8 collective-permute-done
  12.6 0.0 copy-done
  12.6 1.7 opening.1
  14.3 31.0 %all_to_all.48.arrived = f32[128,8,256]{2,1,0:T(8,128)S(1)} all-to-all(f32[128,8,256]{2,1,0:T(8,128)S(1)} %get-tuple-element.25), channel_id=1, replica_groups=mesh['tm_0'=4,'tm_1'=4,'tm_2'=2,'tm_3'=2,'space'=2] {'tm_0','tm_1','tm_2..., dimensions={0} | all-to-all | bytes 2097152 | tf_op jit(solution)/shard_map/all_to_all | solution.py:411
  45.3 2.1 cells.4
  47.5 22.9 %all_to_all.49.block = f32[128,8,256]{2,1,0:T(8,128)S(1)} all-to-all(f32[128,8,256]{2,1,0:T(8,128)S(1)} %get-tuple-element.26), channel_id=1, replica_groups=mesh['tm_0'=4,'tm_1'=4,'tm_2'=2,'tm_3'=2,'space'=2] {'tm_0','tm_1','tm_2..., dimensions={0} | all-to-all | bytes 2097152 | tf_op jit(solution)/shard_map/all_to_all | solution.py:411
  70.4 3.1 %modes.3 = (f32[64,8,512]{2,1,0:T(8,128)S(1)}, f32[8,512]{1,0:T(8,128)S(1)}, f32[128,8,256]{2,1,0:T(8,128)S(1)}) custom-call(f32[128,8,256]{2,1,0:T(8,128)S(1)} %all_to_all.49.block, f32[8,512]{1,0:T(8,128)S(1)} %add_multiply_fusion.tangent, bf16[2,3,512,256]{3,2,1,0:T(8,128)(2,1)S(1)} %copy-done, f32[8,512]{1,0:T(8,128)S(1)} %get-tuple-element.27.earlier.w0, ...), custom_call_target="tpu_custom_call" | custom-call | tf_op jit(solution)/shard_map/modes/pallas_call | solution.py:69
  73.5 22.9 %all_to_all.50.arrived = f32[128,8,256]{2,1,0:T(8,128)S(1)} all-to-all(f32[128,8,256]{2,1,0:T(8,128)S(1)} %get-tuple-element.29), channel_id=1, replica_groups=mesh['tm_0'=4,'tm_1'=4,'tm_2'=2,'tm_3'=2,'space'=2] {'tm_0','tm_1','tm_2..., dimensions={0} | all-to-all | bytes 2097152 | tf_op jit(solution)/shard_map/all_to_all | solution.py:411
  96.4 2.1 cells.5
  98.6 22.9 %all_to_all.51.block = f32[128,8,256]{2,1,0:T(8,128)S(1)} all-to-all(f32[128,8,256]{2,1,0:T(8,128)S(1)} %get-tuple-element.30), channel_id=1, replica_groups=mesh['tm_0'=4,'tm_1'=4,'tm_2'=2,'tm_3'=2,'space'=2] {'tm_0','tm_1','tm_2..., dimensions={0} | all-to-all | bytes 2097152 | tf_op jit(solution)/shard_map/all_to_all | solution.py:411
  121.5 3.1 %modes.4 = (f32[64,8,512]{2,1,0:T(8,128)S(1)}, f32[8,512]{1,0:T(8,128)S(1)}, f32[128,8,256]{2,1,0:T(8,128)S(1)}) custom-call(f32[128,8,256]{2,1,0:T(8,128)S(1)} %all_to_all.51.block, f32[8,512]{1,0:T(8,128)S(1)} %add_multiply_fusion.tangent, bf16[2,3,512,256]{3,2,1,0:T(8,128)(2,1)S(1)} %copy-done, f32[64,8,512]{2,1,0:T(8,128)S(1)} %get-tuple-element.31.earlier.w1, ...), custom_call_target="tpu_custom_call" | custom-call | tf_op jit(solution)/shard_map/modes/pallas_call | solution.py:69
  124.6 22.9 %all_to_all.52.arrived = f32[128,8,256]{2,1,0:T(8,128)S(1)} all-to-all(f32[128,8,256]{2,1,0:T(8,128)S(1)} %get-tuple-element.33), channel_id=1, replica_groups=mesh['tm_0'=4,'tm_1'=4,'tm_2'=2,'tm_3'=2,'space'=2] {'tm_0','tm_1','tm_2..., dimensions={0} | all-to-all | bytes 2097152 | tf_op jit(solution)/shard_map/all_to_all | solution.py:411
  147.6 2.1 cells.6
  149.7 22.9 %all_to_all.53.block = f32[128,8,256]{2,1,0:T(8,128)S(1)} all-to-all(f32[128,8,256]{2,1,0:T(8,128)S(1)} %get-tuple-element.34), channel_id=1, replica_groups=mesh['tm_0'=4,'tm_1'=4,'tm_2'=2,'tm_3'=2,'space'=2] {'tm_0','tm_1','tm_2..., dimensions={0} | all-to-all | bytes 2097152 | tf_op jit(solution)/shard_map/all_to_all | solution.py:411
  172.7 3.1 %modes.5 = (f32[64,8,512]{2,1,0:T(8,128)S(1)}, f32[8,512]{1,0:T(8,128)S(1)}, f32[128,8,256]{2,1,0:T(8,128)S(1)}) custom-call(f32[128,8,256]{2,1,0:T(8,128)S(1)} %all_to_all.53.block, f32[8,512]{1,0:T(8,128)S(1)} %add_multiply_fusion.tangent, bf16[2,3,512,256]{3,2,1,0:T(8,128)(2,1)S(1)} %copy-done, f32[64,8,512]{2,1,0:T(8,128)S(1)} %get-tuple-element.35.earlier.w2, ...), custom_call_target="tpu_custom_call" | custom-call | tf_op jit(solution)/shard_map/modes/pallas_call | solution.py:69
  175.8 22.9 %all_to_all.54.arrived = f32[128,8,256]{2,1,0:T(8,128)S(1)} all-to-all(f32[128,8,256]{2,1,0:T(8,128)S(1)} %get-tuple-element.37), channel_id=1, replica_groups=mesh['tm_0'=4,'tm_1'=4,'tm_2'=2,'tm_3'=2,'space'=2] {'tm_0','tm_1','tm_2..., dimensions={0} | all-to-all | bytes 2097152 | tf_op jit(solution)/shard_map/all_to_all | solution.py:411
  198.7 2.1 cells.7
  200.9 22.9 %all_to_all.55.block = f32[128,8,256]{2,1,0:T(8,128)S(1)} all-to-all(f32[128,8,256]{2,1,0:T(8,128)S(1)} %get-tuple-element.38), channel_id=1, replica_groups=mesh['tm_0'=4,'tm_1'=4,'tm_2'=2,'tm_3'=2,'space'=2] {'tm_0','tm_1','tm_2..., dimensions={0} | all-to-all | bytes 2097152 | tf_op jit(solution)/shard_map/all_to_all | solution.py:411
  223.8 2.0 products.1
  225.9 13.4 %all_to_all.56 = f32[128,1,128]{2,1,0:T(1,128)S(1)} all-to-all(f32[128,1,128]{2,1,0:T(1,128)S(1)} %broadcast_in_dim.2), channel_id=1, replica_groups=mesh['tm_0'=4,'tm_1'=4,'tm_2'=2,'tm_3'=2,'space'=2] {'tm_0','tm_1','tm_2..., dimensions={0} | all-to-all | bytes 131072 | tf_op jit(solution)/shard_map/all_to_all | solution.py:411
  239.3 1.5 combine.1
  (15 shorter events, 0.2 us)
Async XLA Ops:
  0.0 2.6 %copy-start.2 = (f32[2,256,512]{2,1,0:T(8,128)S(1)}, f32[2,256,512]{2,1,0:T(8,128)}, u32[]{:S(2)}) copy-start(f32[2,256,512]{2,1,0:T(8,128)} %param.4) | copy-start | bytes 3145732
  2.9 1.0 copy-start.1
  5.1 7.5 %copy-start = (bf16[2,3,512,256]{3,2,1,0:T(8,128)(2,1)S(1)}, bf16[2,3,512,256]{3,2,1,0:T(8,128)(2,1)}, u32[]{:S(2)}) copy-start(bf16[2,3,512,256]{3,2,1,0:T(8,128)(2,1)} %constant.112.clone.table) | copy-start | bytes 4718596
  7.8 4.8 %collective-permute-start = (f32[2,8,256]{2,1,0:T(8,128)S(1)}, f32[2,8,256]{2,1,0:T(8,128)S(1)}, u32[]{:S(2)}, u32[]{:S(2)}) collective-permute-start(f32[2,8,256]{2,1,0:T(8,128)S(1)} %reshape.69), channel_id=1, source_target_pairs={{0,1},{1,0},{2,3},{3,2},{4,5},{5,4},{6,7},{7,6},{8,9},{9,8},{10,11... | collective-permute-start | bytes 49160 | tf_op jit(solution)/shard_map/ppermute | solution.py:440

commit v3 on v2

--- a/solution.py
+++ b/solution.py
@@ -22,7 +22,6 @@
 alpha = 0.4
 shift = alpha * alpha / (1.0 - alpha * alpha)
 scale = alpha / (1.0 - alpha * alpha)
-highest = lax.Precision.HIGHEST
 f32 = jnp.float32
 bf16 = jnp.bfloat16
 
@@ -54,6 +53,10 @@
     return jnp.dot(left, right, preferred_element_type=f32)
 
 
+def dot_last(left, right):
+    return lax.dot_general(left, right, (((1,), (1,)), ((), ())), preferred_element_type=f32)
+
+
 def table_times(table, which, value):
     high, low = halves(value)
     return dot(table[0, which], high) + dot(table[1, which], high) + dot(table[0, which], low)
@@ -64,15 +67,15 @@
     return dot(high, table[0, which]) + dot(high, table[1, which]) + dot(low, table[0, which])
 
 
-def call(body, out_shape, name, scratch, *operands):
+def call(body, out_shape, name, scratch, *operands, copied=0):
     inside = pl.BlockSpec(memory_space=pltpu.VMEM)
     return pl.pallas_call(
         body,
         out_shape=out_shape,
-        in_specs=[inside] * len(operands),
+        in_specs=[pl.BlockSpec(memory_space=pltpu.HBM)] * copied + [inside] * (len(operands) - copied),
         out_specs=jax.tree.map(lambda unused: inside, out_shape),
         scratch_shapes=scratch,
-        compiler_params=pltpu.CompilerParams(vmem_limit_bytes=24 << 20),
+        compiler_params=pltpu.CompilerParams(vmem_limit_bytes=(63 if copied else 24) << 20),
         name=name,
     )(*operands)
 
@@ -169,15 +172,6 @@
     return left[0] * right[0] - left[1] * right[1], left[0] * right[1] + left[1] * right[0]
 
 
-def wrap_factor(turn):
-    side = signs((8, NX), -1.0, 1.0)
-    power = turn
-    for unused in range(6):
-        power = multiplied(power, power)
-        power = (power[0], power[1])
-    return power, side
-
-
 def rows_forward(block, count, table, into):
     pair = block.reshape(count, 2, 8, HALF)
     first, second = pair[:, 0], pair[:, 1]
@@ -214,27 +208,68 @@
     return (real * rest - imag * imag) * inverse, (imag * rest + real * imag) * inverse * side
 
 
-def next_power(power, turn, conjugate):
-    sign = -1.0 if conjugate else 1.0
-    real = power[0] * turn[0] - sign * power[1] * turn[1]
-    imag = sign * power[0] * turn[1] + power[1] * turn[0]
-    return real, imag
-
-
 NORMAL = 1.0 / (NX * NY)
 
 
-def replay(turn, offset, summed, modes):
-    def step(n, power):
-        value = offset if summed is None else offset + summed[n]
-        modes[n] = NORMAL * product_of(power[0], power[1], value)
-        return next_power(power, turn, False)
-
-    one = jnp.ones((8, NX), f32)
-    lax.fori_loop(0, TIME, step, (one, jnp.zeros((8, NX), f32)), unroll=4)
-
-
-def opening_kernel(block, tangent, table, vector, offset, sent, spectrum, modes):
+def fetched(sources, targets, arrivals):
+    pieces = []
+    for source, target in zip(sources, targets):
+        for start in range(0, HALF, 64):
+            if len(source.shape) == 3:
+                pieces += [(source.at[c, pl.ds(start, 64)], target.at[c, pl.ds(start, 64)]) for c in range(2)]
+            else:
+                pieces.append((source.at[pl.ds(start, 64)], target.at[pl.ds(start, 64)]))
+    copies = [
+        pltpu.make_async_copy(source, target, arrivals.at[place])
+        for place, (source, target) in enumerate(pieces)
+    ]
+    for copy in copies:
+        copy.start()
+    for copy in copies:
+        copy.wait()
+
+
+def columns_kernel(far_field, far_phase, far_absorb, trig, mine, theirs, field, phase, absorb, arrivals):
+    fetched((far_field, far_phase, far_absorb), (field, phase, absorb), arrivals)
+    real, imag = field[0], field[1]
+    damped_real = 0.5 * (absorb[...] * real - phase[...] * imag)
+    damped_imag = 0.5 * (absorb[...] * imag + phase[...] * real)
+    high, low = halves(jnp.concatenate([real, imag, damped_real, damped_imag], axis=0))
+    trig_high, trig_low = halves(trig[...])
+    product = dot_last(trig_high, high) + dot_last(trig_low, high) + dot_last(trig_high, low)
+    upper = upper_rows((8, 1))
+    for place in range(2):
+        start = 2 * place * HALF
+        first = product[:, start : start + HALF]
+        second = product[:, start + HALF : start + 2 * HALF]
+        real = first[:8] + second[8:]
+        imag = second[:8] - first[8:]
+        mine[place] = jnp.where(upper, real, swapped(imag))
+        theirs[place] = jnp.where(upper, swapped(real), imag)
+
+
+def columns_of(field, phase, absorb, trig):
+    operands = (field, phase, absorb, trig)
+    scratch = (
+        pltpu.VMEM((2, HALF, NY), f32),
+        pltpu.VMEM((HALF, NY), f32),
+        pltpu.VMEM((HALF, NY), f32),
+        pltpu.SemaphoreType.DMA((16,)),
+    )
+    shapes = (array(2, 8, HALF), array(2, 8, HALF))
+    return call(columns_kernel, shapes, "columns", scratch, *operands, copied=3)
+
+
+def turning_kernel(phase, absorb, damping):
+    damping[0] = (0.5 / scale) * absorb[...].T
+    damping[1] = (0.5 / scale) * phase[...].T
+
+
+def turned(phase, absorb):
+    return call(turning_kernel, array(2, NY, HALF), "turning", (), phase, absorb)
+
+
+def opening_kernel(block, tangent, table, vector, offset, sent, powers, spectrum, modes):
     rows_forward(block[...], 2, table, spectrum)
     slope = tangent[...]
     turn_real, turn_imag, gain_real, gain_imag = rotation(slope)
@@ -243,80 +278,90 @@
     vector[...] = product_of(1.0, -slope * side, wave) - damped
     value = product_of(turn_real, turn_imag, wave) - product_of(gain_real, gain_imag, damped)
     wrap = product_of(*closing((turn_real, turn_imag)), value)
-    offset[...] = wrap
-    replay((turn_real, turn_imag), wrap + value, None, modes)
+    offset[...] = product_of(1.0, slope * side, wrap)
+    start = NORMAL * (wrap + value)
+
+    def step(n, power):
+        real, imag = power
+        powers[n, 0] = real
+        powers[n, 1] = imag
+        modes[n] = product_of(real, imag, start)
+        return real * turn_real - imag * turn_imag, real * turn_imag + imag * turn_real
+
+    one = jnp.ones((8, NX), f32)
+    lax.fori_loop(0, TIME, step, (one, jnp.zeros((8, NX), f32)), unroll=4)
     rows_inverse(modes, table, sent)
 
 
 def opening(block, tangent, table):
-    shapes = (array(8, NX), array(8, NX), array(DEVICES, 8, HALF))
+    shapes = (
+        array(8, NX),
+        array(8, NX),
+        array(DEVICES, 8, HALF),
+        array(TIME, 2, 8, NX),
+    )
     scratch = (pltpu.VMEM((2, 8, NX), f32), pltpu.VMEM((TIME, 8, NX), f32))
     return call(opening_kernel, shapes, "opening", scratch, block, tangent, table)
 
 
-def image_step(n, before, spectrum, slope_signed, offset, earlier):
-    here = spectrum[n]
-    value = here + before
-    if earlier is not None:
-        value = value - shift * earlier[n]
-    return here, value * (1.0 / scale)
-
-
-def wrapped_term(slope, offset):
-    side = signs((8, NX), -1.0, 1.0)
-    return offset + slope * side * swapped(offset)
-
-
 def modes_kernel_of(first):
-    def body(block, tangent, table, earlier, offset_in, vector, offset, sent, spectrum, summed):
-        rows_forward(block[...], TIME, table, spectrum)
+    def body(block, tangent, table, powers, earlier, wrap_in, vector, wrap_out, sent, modes, sums):
+        rows_forward(block[...], TIME, table, modes)
         slope = tangent[...]
         turn_real, turn_imag, gain_real, gain_imag = rotation(slope)
-        turn = (turn_real, turn_imag)
-        wrap = wrapped_term(slope, offset_in[...])
+        before = (1.0 / scale) * wrap_in[...]
         if first:
-            wrap = wrap - shift * earlier[...]
+            before = before - alpha * earlier[...]
 
         def step(n, carry):
-            before, total, power = carry
-            here, value = image_step(n, before, spectrum, None, None, None if first else earlier)
+            before, total = carry
+            here = modes[n]
+            value = here + before
+            if not first:
+                value = value - alpha * earlier[n]
             vector[n] = value
-            total = total + product_of(power[0], power[1], value)
-            summed[n] = total
-            return here, total, next_power(power, turn, True)
+            total = total + product_of(powers[n, 0], -powers[n, 1], value)
+            sums[n] = total
+            return here, total
 
         zero = jnp.zeros((8, NX), f32)
-        unused, total, power = lax.fori_loop(
-            0, TIME, step, (wrap, zero, (gain_real, gain_imag)), unroll=4
-        )
-        wrap = product_of(*closing(turn), total)
-        offset[...] = wrap
-        replay(turn, wrap, summed, spectrum)
-        rows_inverse(spectrum, table, sent)
+        unused, total = lax.fori_loop(0, TIME, step, (before, zero), unroll=4)
+        wrap = product_of(*closing((turn_real, turn_imag)), total)
+        wrap_out[...] = wrap
+        gain_real, gain_imag = NORMAL * gain_real, NORMAL * gain_imag
+
+        def replay(n, carry):
+            value = product_of(gain_real, gain_imag, wrap + sums[n])
+            modes[n] = product_of(powers[n, 0], powers[n, 1], value)
+            return carry
+
+        lax.fori_loop(0, TIME, replay, 0, unroll=4)
+        rows_inverse(modes, table, sent)
 
     return body
 
 
-def on_modes(block, tangent, table, earlier, offset_in, first):
+def on_modes(block, tangent, table, powers, earlier, wrap, first):
     shapes = (array(TIME, 8, NX), array(8, NX), array(DEVICES, 8, HALF))
     scratch = (pltpu.VMEM((TIME, 8, NX), f32), pltpu.VMEM((TIME, 8, NX), f32))
     body = modes_kernel_of(first)
-    return call(body, shapes, "modes", scratch, block, tangent, table, earlier, offset_in)
+    operands = (block, tangent, table, powers, earlier, wrap)
+    return call(body, shapes, "modes", scratch, *operands)
 
 
 PAIRS = [(i, j) for i in range(1, ITERS + 1) for j in range(i, ITERS + 1)]
 
 
-def products_kernel(block, tangent, table, w0, w1, w2, w3, offset_in, totals, spectrum):
+def products_kernel(block, table, w0, w1, w2, w3, wrap, totals, spectrum):
     rows_forward(block[...], TIME, table, spectrum)
-    wrap = wrapped_term(tangent[...], offset_in[...])
 
     def narrowed(value):
         return value[:, 0:128] + value[:, 128:256] + value[:, 256:384] + value[:, 384:512]
 
     def step(n, carry):
         before, sums = carry
-        here, value = image_step(n, before, spectrum, None, None, w3)
+        here = spectrum[n]
+        value = here + before - alpha * w3[n]
         vectors = (None, w1[n], w2[n], w3[n], value)
         sums = tuple(
             total + narrowed(vectors[i] * vectors[j]) for total, (i, j) in zip(sums, PAIRS)
@@ -324,7 +369,8 @@
         return here, sums
 
     start = w0[...]
-    here, first = image_step(0, wrap, spectrum, None, None, w3)
+    here = spectrum[0]
+    first = here + (1.0 / scale) * wrap[...] - alpha * w3[0]
     heads = (start, w1[0], w2[0], w3[0], first)
     sums = tuple(narrowed(heads[i] * heads[j]) for i, j in PAIRS)
     unused, sums = lax.fori_loop(1, TIME, step, (here, sums), unroll=3)
@@ -337,9 +383,9 @@
     totals[...] = packed
 
 
-def products(block, tangent, table, vectors, offset_in):
+def products(block, table, vectors, wrap):
     scratch = (pltpu.VMEM((TIME, 8, NX), f32),)
-    operands = (block, tangent, table, *vectors, offset_in)
+    operands = (block, table, *vectors, wrap)
     return call(products_kernel, array(1, 128), "products", scratch, *operands)
 
 
@@ -420,36 +466,26 @@
     step = lax.axis_index(TM)
     half = lax.axis_index("space")
     table = jnp.asarray(TABLES)
-    damping = 0.5 * jnp.stack([absorb, phase])
-    modes = column_modes(8 * step, 8)
-    turns = modes[:, None] * jnp.arange(NY, dtype=jnp.int32)[None, :] % NY
+    own = column_modes(4 * (2 * step + half), 4)
+    other = column_modes(4 * (2 * (step ^ 2) + 1 - half), 4)
+    turns = jnp.concatenate([own, other])[:, None] * jnp.arange(NY, dtype=jnp.int32)[None, :] % NY
     angle = turns.astype(f32) * (2.0 * math.pi / NY)
-    damped = jnp.stack(
-        [
-            damping[0] * u_init[0] - damping[1] * u_init[1],
-            damping[0] * u_init[1] + damping[1] * u_init[0],
-        ]
-    )
-    fields = jnp.stack([u_init, damped])
-    cosine = jnp.einsum("fcxy,ky->fckx", fields, jnp.cos(angle), precision=highest)
-    sine = jnp.einsum("fcxy,ky->fckx", fields, jnp.sin(angle), precision=highest)
-    columns = jnp.stack([cosine[:, 0] + sine[:, 1], cosine[:, 1] - sine[:, 0]], axis=1)
-    columns = columns.reshape(2, 2, 2, 4, HALF)
-    mine = lax.dynamic_index_in_dim(columns, half, 2, keepdims=False).reshape(2, 8, HALF)
-    theirs = lax.dynamic_index_in_dim(columns, 1 - half, 2, keepdims=False).reshape(2, 8, HALF)
-    theirs = lax.ppermute(theirs, "space", [(0, 1), (1, 0)])
+    trig = jnp.concatenate([jnp.cos(angle), jnp.sin(angle)])
+    mine, theirs = columns_of(u_init, phase, absorb, trig)
+    theirs = lax.ppermute(theirs, ("tm_2", "space"), [(0, 3), (1, 2), (2, 1), (3, 0)])
     block = jnp.where(
         half == 0, jnp.stack([mine, theirs], axis=1), jnp.stack([theirs, mine], axis=1)
     ).reshape(4, 8, HALF)
-    own = column_modes(8 * step + 4 * half, 4).astype(f32)
+    own = own.astype(f32)
     rows = jnp.arange(HALF, dtype=jnp.int32)
     rows = jnp.concatenate([2 * rows, 2 * rows + 1]).astype(f32)
     symbol_y = 4.0 * jnp.sin(own * (math.pi / NY)) ** 2
     symbol_x = 4.0 * jnp.sin(rows * (math.pi / NX)) ** 2
     tangent = (0.5 * tau) * (jnp.concatenate([symbol_y, symbol_y])[:, None] + symbol_x[None, :])
-    damping = damping.swapaxes(1, 2)
-
-    vector, offset, sent = opening(block, tangent, table)
+    damping = turned(phase, absorb)
+    block, damping = lax.optimization_barrier((block, damping))
+
+    vector, wrap, sent, powers = opening(block, tangent, table)
     vectors = [vector]
     found = []
     for column in range(ITERS):
@@ -457,11 +493,11 @@
         found.append(field)
         arrived = exchange(sent)
         if column + 1 < ITERS:
-            vector, offset, sent = on_modes(
-                arrived, tangent, table, vectors[-1], offset, column == 0
+            vector, wrap, sent = on_modes(
+                arrived, tangent, table, powers, vectors[-1], wrap, column == 0
             )
             vectors.append(vector)
-    totals = products(arrived, tangent, table, vectors, offset)
+    totals = products(arrived, table, vectors, wrap)
     return combine(exchange(jnp.broadcast_to(totals, (DEVICES, 128))), found)
 
 

time: 241 us -> 237 us (0.983)
  matrix products: 3.78 us -> 0 us
  Pallas kernels: 23.1 us -> 26.3 us
    dot_general x2 -> x0, matrix products: 3.78 us -> none  [the longest x1 2.57 us: shards(): jnp.einsum('fcxy,ky->fckx', fields, jnp.cos(angle), precision=highest)]
    pallas_call x10 -> x12, Pallas kernels: 23.1 us -> 26.3 us  [call(): pl.pallas_call(body, out_shape=out_shape, in_specs=[pl.BlockSpec(memory_s...]
  transfers between devices with their start and end apart: 1 -> 1, of which waited for: 1 -> 0; matrix products, arithmetic and copies ran while one was open for 0% -> 0% of each run, Pallas kernels for 0% -> 0%
where the time goes in v3:
time: 237 us; the launch traced here: 236 us
  blocking collectives  204 us (86%)
  Pallas kernels  26.3 us (11%)
  starting transfers between devices  3.38 us (1%)
    all_to_all x9, blocking collectives, exchange(): lax.all_to_all(value, TM_SPACE, split_axis=0, concat_axis=0, tiled=True)  204 us
    pallas_call x12, Pallas kernels, call(): pl.pallas_call(body, out_shape=out_shape, in_specs=[pl.BlockSpec(memory_s...  26.3 us
  transfers between devices with their start and end apart: 1, of which 0 were waited for; matrix products, arithmetic and copies ran while one was open for 0% of the time, Pallas kernels for 0%

profile of v3, /device:TPU:1, one launch (start us, length us, event | category | flops | bytes accessed | tf_op | source)
XLA Modules:
  0.0 236.4 jit_solution(18013962164756533571)
XLA Ops:
  0.0 0.0 copy-start.1
  0.0 0.1 pad_add_fusion
  0.1 0.2 fusion.7
  0.3 0.6 pad_maximum_fusion.trig
  0.9 4.0 %columns.1 = (f32[2,8,256]{2,1,0:T(8,128)}, f32[2,8,256]{2,1,0:T(8,128)}) custom-call(f32[2,256,512]{2,1,0:T(8,128)} %far_field.1, f32[256,512]{1,0:T(8,128)} %phase.1, f32[256,512]{1,0:T(8,128)} %absorb.1, f32[16,512]{1,0:T(8,128)} %pad_maximum_fusion.trig), custom_call_target="tpu_custom_call" | custom-call | tf_op jit(solution)/shard_map/columns/pallas_call | solution.py:72
  4.9 0.0 copy-start
  4.9 3.4 %collective-permute-start = (f32[2,8,256]{2,1,0:T(8,128)}, f32[2,8,256]{2,1,0:T(8,128)S(1)}, u32[]{:S(2)}, u32[]{:S(2)}) collective-permute-start(f32[2,8,256]{2,1,0:T(8,128)} %get-tuple-element.31), channel_id=1, source_target_pairs={{0,5},{1,4},{4,1},{5,0},{2,7},{3,6},{6,3},{7,2},{8,13},{9,12},{12,... | collective-permute-start | bytes 49160 | tf_op jit(solution)/shard_map/ppermute | solution.py:475
  8.3 0.1 multiply_multiply_fusion
  8.4 0.1 pad_maximum_fusion.1
  8.5 0.1 add_multiply_fusion.tangent
  8.6 0.0 copy-done.1
  8.6 0.0 copy-start.2
  8.6 1.0 copy-done.2
  9.6 0.0 copy-start.3
  9.6 0.3 turning.1.damping
  10.0 0.0 collective-permute-done
  10.0 0.4 copy-done.3
  10.4 0.0 copy-done
  10.4 1.7 opening.1
  12.0 30.0 %all_to_all.48.arrived = f32[128,8,256]{2,1,0:T(8,128)S(1)} all-to-all(f32[128,8,256]{2,1,0:T(8,128)S(1)} %get-tuple-element.33), channel_id=1, replica_groups=mesh['tm_0'=4,'tm_1'=4,'tm_2'=2,'tm_3'=2,'space'=2] {'tm_0','tm_1','tm_2..., dimensions={0} | all-to-all | bytes 2097152 | tf_op jit(solution)/shard_map/all_to_all | solution.py:457
  42.1 2.1 cells.4
  44.2 22.9 %all_to_all.49.block = f32[128,8,256]{2,1,0:T(8,128)S(1)} all-to-all(f32[128,8,256]{2,1,0:T(8,128)S(1)} %get-tuple-element.35), channel_id=1, replica_groups=mesh['tm_0'=4,'tm_1'=4,'tm_2'=2,'tm_3'=2,'space'=2] {'tm_0','tm_1','tm_2..., dimensions={0} | all-to-all | bytes 2097152 | tf_op jit(solution)/shard_map/all_to_all | solution.py:457
  67.2 2.7 %modes.3 = (f32[64,8,512]{2,1,0:T(8,128)S(1)}, f32[8,512]{1,0:T(8,128)S(1)}, f32[128,8,256]{2,1,0:T(8,128)S(1)}) custom-call(f32[128,8,256]{2,1,0:T(8,128)S(1)} %all_to_all.49.block, f32[8,512]{1,0:T(8,128)S(1)} %add_multiply_fusion.tangent, bf16[2,3,512,256]{3,2,1,0:T(8,128)(2,1)S(1)} %copy-done, f32[64,2,8,512]{3,2,1,0:T(8,128)S(1)} %get-tuple-element.36.powers, ...), custom_call_target="tpu_custom_call" | custom-call | tf_op jit(solution)/shard_map/modes/pallas_call | solution.py:72
  69.9 22.9 %all_to_all.50.arrived = f32[128,8,256]{2,1,0:T(8,128)S(1)} all-to-all(f32[128,8,256]{2,1,0:T(8,128)S(1)} %get-tuple-element.39), channel_id=1, replica_groups=mesh['tm_0'=4,'tm_1'=4,'tm_2'=2,'tm_3'=2,'space'=2] {'tm_0','tm_1','tm_2..., dimensions={0} | all-to-all | bytes 2097152 | tf_op jit(solution)/shard_map/all_to_all | solution.py:457
  92.8 2.1 cells.5
  95.0 22.9 %all_to_all.51.block = f32[128,8,256]{2,1,0:T(8,128)S(1)} all-to-all(f32[128,8,256]{2,1,0:T(8,128)S(1)} %get-tuple-element.40), channel_id=1, replica_groups=mesh['tm_0'=4,'tm_1'=4,'tm_2'=2,'tm_3'=2,'space'=2] {'tm_0','tm_1','tm_2..., dimensions={0} | all-to-all | bytes 2097152 | tf_op jit(solution)/shard_map/all_to_all | solution.py:457
  117.9 2.8 %modes.4 = (f32[64,8,512]{2,1,0:T(8,128)S(1)}, f32[8,512]{1,0:T(8,128)S(1)}, f32[128,8,256]{2,1,0:T(8,128)S(1)}) custom-call(f32[128,8,256]{2,1,0:T(8,128)S(1)} %all_to_all.51.block, f32[8,512]{1,0:T(8,128)S(1)} %add_multiply_fusion.tangent, bf16[2,3,512,256]{3,2,1,0:T(8,128)(2,1)S(1)} %copy-done, f32[64,2,8,512]{3,2,1,0:T(8,128)S(1)} %get-tuple-element.36.powers, ...), custom_call_target="tpu_custom_call" | custom-call | tf_op jit(solution)/shard_map/modes/pallas_call | solution.py:72
  120.7 22.9 %all_to_all.52.arrived = f32[128,8,256]{2,1,0:T(8,128)S(1)} all-to-all(f32[128,8,256]{2,1,0:T(8,128)S(1)} %get-tuple-element.43), channel_id=1, replica_groups=mesh['tm_0'=4,'tm_1'=4,'tm_2'=2,'tm_3'=2,'space'=2] {'tm_0','tm_1','tm_2..., dimensions={0} | all-to-all | bytes 2097152 | tf_op jit(solution)/shard_map/all_to_all | solution.py:457
  143.6 2.1 cells.6
  145.8 22.9 %all_to_all.53.block = f32[128,8,256]{2,1,0:T(8,128)S(1)} all-to-all(f32[128,8,256]{2,1,0:T(8,128)S(1)} %get-tuple-element.44), channel_id=1, replica_groups=mesh['tm_0'=4,'tm_1'=4,'tm_2'=2,'tm_3'=2,'space'=2] {'tm_0','tm_1','tm_2..., dimensions={0} | all-to-all | bytes 2097152 | tf_op jit(solution)/shard_map/all_to_all | solution.py:457
  168.7 2.8 %modes.5 = (f32[64,8,512]{2,1,0:T(8,128)S(1)}, f32[8,512]{1,0:T(8,128)S(1)}, f32[128,8,256]{2,1,0:T(8,128)S(1)}) custom-call(f32[128,8,256]{2,1,0:T(8,128)S(1)} %all_to_all.53.block, f32[8,512]{1,0:T(8,128)S(1)} %add_multiply_fusion.tangent, bf16[2,3,512,256]{3,2,1,0:T(8,128)(2,1)S(1)} %copy-done, f32[64,2,8,512]{3,2,1,0:T(8,128)S(1)} %get-tuple-element.36.powers, ...), custom_call_target="tpu_custom_call" | custom-call | tf_op jit(solution)/shard_map/modes/pallas_call | solution.py:72
  171.5 22.9 %all_to_all.54.arrived = f32[128,8,256]{2,1,0:T(8,128)S(1)} all-to-all(f32[128,8,256]{2,1,0:T(8,128)S(1)} %get-tuple-element.47), channel_id=1, replica_groups=mesh['tm_0'=4,'tm_1'=4,'tm_2'=2,'tm_3'=2,'space'=2] {'tm_0','tm_1','tm_2..., dimensions={0} | all-to-all | bytes 2097152 | tf_op jit(solution)/shard_map/all_to_all | solution.py:457
  194.4 2.1 cells.7
  196.6 22.9 %all_to_all.55.block = f32[128,8,256]{2,1,0:T(8,128)S(1)} all-to-all(f32[128,8,256]{2,1,0:T(8,128)S(1)} %get-tuple-element.48), channel_id=1, replica_groups=mesh['tm_0'=4,'tm_1'=4,'tm_2'=2,'tm_3'=2,'space'=2] {'tm_0','tm_1','tm_2..., dimensions={0} | all-to-all | bytes 2097152 | tf_op jit(solution)/shard_map/all_to_all | solution.py:457
  219.5 2.0 products.1
  221.5 13.4 %all_to_all.56 = f32[128,1,128]{2,1,0:T(1,128)S(1)} all-to-all(f32[128,1,128]{2,1,0:T(1,128)S(1)} %broadcast_in_dim.2), channel_id=1, replica_groups=mesh['tm_0'=4,'tm_1'=4,'tm_2'=2,'tm_3'=2,'space'=2] {'tm_0','tm_1','tm_2..., dimensions={0} | all-to-all | bytes 131072 | tf_op jit(solution)/shard_map/all_to_all | solution.py:457
  234.9 1.5 combine.1
  (6 shorter events, 0.1 us)
Async XLA Ops:
  0.0 8.6 %copy-start.1 = (f32[256,512]{1,0:T(8,128)S(1)}, f32[256,512]{1,0:T(8,128)}, u32[]{:S(2)}) copy-start(f32[256,512]{1,0:T(8,128)} %phase.1) | copy-start | bytes 1572868
  4.9 5.4 %copy-start = (bf16[2,3,512,256]{3,2,1,0:T(8,128)(2,1)S(1)}, bf16[2,3,512,256]{3,2,1,0:T(8,128)(2,1)}, u32[]{:S(2)}) copy-start(bf16[2,3,512,256]{3,2,1,0:T(8,128)(2,1)} %constant.95.clone.table) | copy-start | bytes 4718596
  4.9 5.0 %collective-permute-start = (f32[2,8,256]{2,1,0:T(8,128)}, f32[2,8,256]{2,1,0:T(8,128)S(1)}, u32[]{:S(2)}, u32[]{:S(2)}) collective-permute-start(f32[2,8,256]{2,1,0:T(8,128)} %get-tuple-element.31), channel_id=1, source_target_pairs={{0,5},{1,4},{4,1},{5,0},{2,7},{3,6},{6,3},{7,2},{8,13},{9,12},{12,... | collective-permute-start | bytes 49160 | tf_op jit(solution)/shard_map/ppermute | solution.py:475
  8.6 1.0 copy-start.2
  9.6 0.7 copy-start.3

commit v4 on v3

--- a/solution.py
+++ b/solution.py
@@ -12,6 +12,7 @@
 NX = 512
 NY = 512
 HALF = 256
+LANES = 128
 TIME = 64
 ITERS = 4
 DEVICES = 128
@@ -75,7 +76,7 @@
         in_specs=[pl.BlockSpec(memory_space=pltpu.HBM)] * copied + [inside] * (len(operands) - copied),
         out_specs=jax.tree.map(lambda unused: inside, out_shape),
         scratch_shapes=scratch,
-        compiler_params=pltpu.CompilerParams(vmem_limit_bytes=(63 if copied else 24) << 20),
+        compiler_params=pltpu.CompilerParams(vmem_limit_bytes=24 << 20),
         name=name,
     )(*operands)
 
@@ -97,55 +98,54 @@
 
 
 def split_parts(block):
-    pair = block.reshape(32, 2, 8, HALF)
+    pair = block.reshape(32, 2, 8, LANES)
     first, second = pair[:, 0], pair[:, 1]
     upper = upper_rows((1, 8, 1))
     real = jnp.where(upper, first, swapped(second))
     imag = jnp.where(upper, swapped(first), second)
-    return real.reshape(HALF, HALF), imag.reshape(HALF, HALF)
+    return real.reshape(HALF, LANES), imag.reshape(HALF, LANES)
 
 
 def merge_parts(real, imag):
-    real = real.reshape(32, 8, HALF)
-    imag = imag.reshape(32, 8, HALF)
+    real = real.reshape(32, 8, LANES)
+    imag = imag.reshape(32, 8, LANES)
     upper = upper_rows((1, 8, 1))
     first = jnp.where(upper, real, swapped(imag))
     second = jnp.where(upper, swapped(real), imag)
-    return jnp.stack([first, second], axis=1).reshape(64, 8, HALF)
+    return jnp.stack([first, second], axis=1).reshape(64, 8, LANES)
 
 
 def cells_kernel(arrived, damping, table, field, sent):
-    def inverse(part, which):
-        real, imag = split_parts(arrived[pl.ds(part * 64, 64)])
+    def inverse(part, which, lanes):
+        real, imag = split_parts(arrived[pl.ds(part * 64, 64), :, lanes])
         product = table_times(table, which, jnp.concatenate([real, imag], axis=1))
         top, bottom = product[:HALF], product[HALF:]
-        return top[:, :HALF] - bottom[:, HALF:], top[:, HALF:] + bottom[:, :HALF]
-
-    even_real, even_imag = inverse(0, EVEN)
-    odd_real, odd_imag = inverse(1, ODD_T)
-    near = (even_real + odd_real, even_imag + odd_imag)
-    far = (even_real - odd_real, even_imag - odd_imag)
-    damped = []
-    for place, (real, imag) in enumerate((near, far)):
-        rows = pl.ds(place * HALF, HALF)
-        field[0, rows] = real
-        field[1, rows] = imag
-        absorb = damping[0, rows]
-        phase = damping[1, rows]
-        damped.append((absorb * real - phase * imag, absorb * imag + phase * real))
-
-    def forward(part, which, sign):
-        value = jnp.concatenate(
-            [damped[0][0] + sign * damped[1][0], damped[0][1] + sign * damped[1][1]], axis=1
-        )
+        return top[:, :LANES] - bottom[:, LANES:], top[:, LANES:] + bottom[:, :LANES]
+
+    def forward(part, which, value, lanes):
         product = table_times(table, which, value)
         top, bottom = product[:HALF], product[HALF:]
-        sent[pl.ds(part * 64, 64)] = merge_parts(
-            top[:, :HALF] + bottom[:, HALF:], top[:, HALF:] - bottom[:, :HALF]
+        sent[pl.ds(part * 64, 64), :, lanes] = merge_parts(
+            top[:, :LANES] + bottom[:, LANES:], top[:, LANES:] - bottom[:, :LANES]
         )
 
-    forward(0, EVEN, 1.0)
-    forward(1, ODD, -1.0)
+    ranges = [pl.ds(start, LANES) for start in range(0, HALF, LANES)]
+    waves = [(inverse(0, EVEN, lanes), inverse(1, ODD_T, lanes)) for lanes in ranges]
+    for lanes, (even, odd) in zip(ranges, waves):
+        damped = []
+        for place, sign in enumerate((1.0, -1.0)):
+            rows = pl.ds(place * HALF, HALF)
+            real = even[0] + sign * odd[0]
+            imag = even[1] + sign * odd[1]
+            field[0, rows, lanes] = real
+            field[1, rows, lanes] = imag
+            absorb = damping[0, rows, lanes]
+            phase = damping[1, rows, lanes]
+            damped.append(
+                jnp.concatenate([absorb * real - phase * imag, absorb * imag + phase * real], axis=1)
+            )
+        forward(0, EVEN, damped[0] + damped[1], lanes)
+        forward(1, ODD, damped[0] - damped[1], lanes)
 
 
 def on_cells(arrived, damping, table):
@@ -172,23 +172,26 @@
     return left[0] * right[0] - left[1] * right[1], left[0] * right[1] + left[1] * right[0]
 
 
+PARTS = ((EVEN, EVEN, 1.0, pl.ds(0, HALF)), (ODD_T, ODD, -1.0, pl.ds(HALF, HALF)))
+
+
 def rows_forward(block, count, table, into):
     pair = block.reshape(count, 2, 8, HALF)
-    first, second = pair[:, 0], pair[:, 1]
     side = signs((1, 8, 1), 1.0, -1.0)
-    for value, which, start in ((first + second, EVEN, 0), (first - second, ODD_T, HALF)):
+    for which, unused, sign, lanes in PARTS:
+        value = pair[:, 0] + sign * pair[:, 1]
         value = jnp.concatenate([value, side * swapped(value)], axis=2).reshape(8 * count, NX)
-        into[:, :, pl.ds(start, HALF)] = times_table(value, table, which).reshape(count, 8, HALF)
-
-
-def rows_inverse(modes, table, sent):
+        into[:, :, lanes] = times_table(value, table, which).reshape(count, 8, HALF)
+
+
+def row_half(modes, table, which, lanes):
     side = signs((1, 8, 1), -1.0, 1.0)
-    results = []
-    for which, start in ((EVEN, 0), (ODD, HALF)):
-        value = modes[:, :, pl.ds(start, HALF)]
-        value = jnp.concatenate([value, side * swapped(value)], axis=2).reshape(TIME * 8, NX)
-        results.append(times_table(value, table, which).reshape(TIME, 8, HALF))
-    even, odd = results
+    value = modes[:, :, lanes]
+    value = jnp.concatenate([value, side * swapped(value)], axis=2).reshape(TIME * 8, NX)
+    return times_table(value, table, which).reshape(TIME, 8, HALF)
+
+
+def joined(even, odd, sent):
     sent[...] = jnp.stack([even + odd, even - odd], axis=1).reshape(DEVICES, 8, HALF)
 
 
@@ -249,7 +252,8 @@
 
 
 def columns_of(field, phase, absorb, trig):
-    operands = (field, phase, absorb, trig)
+    far = [pltpu.with_memory_space_constraint(value, pltpu.HBM) for value in (field, phase, absorb)]
+    operands = (*far, trig)
     scratch = (
         pltpu.VMEM((2, HALF, NY), f32),
         pltpu.VMEM((HALF, NY), f32),
@@ -290,7 +294,7 @@
 
     one = jnp.ones((8, NX), f32)
     lax.fori_loop(0, TIME, step, (one, jnp.zeros((8, NX), f32)), unroll=4)
-    rows_inverse(modes, table, sent)
+    joined(*[row_half(modes, table, which, lanes) for unused, which, sign, lanes in PARTS], sent)
 
 
 def opening(block, tangent, table):
@@ -309,34 +313,39 @@
         rows_forward(block[...], TIME, table, modes)
         slope = tangent[...]
         turn_real, turn_imag, gain_real, gain_imag = rotation(slope)
-        before = (1.0 / scale) * wrap_in[...]
+        start = (1.0 / scale) * wrap_in[...]
         if first:
-            before = before - alpha * earlier[...]
-
-        def step(n, carry):
-            before, total = carry
-            here = modes[n]
-            value = here + before
-            if not first:
-                value = value - alpha * earlier[n]
-            vector[n] = value
-            total = total + product_of(powers[n, 0], -powers[n, 1], value)
-            sums[n] = total
-            return here, total
-
-        zero = jnp.zeros((8, NX), f32)
-        unused, total = lax.fori_loop(0, TIME, step, (before, zero), unroll=4)
-        wrap = product_of(*closing((turn_real, turn_imag)), total)
-        wrap_out[...] = wrap
+            start = start - alpha * earlier[...]
+        closed = closing((turn_real, turn_imag))
         gain_real, gain_imag = NORMAL * gain_real, NORMAL * gain_imag
-
-        def replay(n, carry):
-            value = product_of(gain_real, gain_imag, wrap + sums[n])
-            modes[n] = product_of(powers[n, 0], powers[n, 1], value)
-            return carry
-
-        lax.fori_loop(0, TIME, replay, 0, unroll=4)
-        rows_inverse(modes, table, sent)
+        wraps = []
+        for part in range(2):
+            lanes = PARTS[part][3]
+            before = start[:, part * HALF : (part + 1) * HALF]
+            total = jnp.zeros((8, HALF), f32)
+            for n in range(TIME):
+                here = modes[n, :, lanes]
+                value = here + before
+                before = here
+                if not first:
+                    value = value - alpha * earlier[n, :, lanes]
+                vector[n, :, lanes] = value
+                total = total + product_of(powers[n, 0, :, lanes], -powers[n, 1, :, lanes], value)
+                sums[n, :, lanes] = total
+            columns = slice(part * HALF, (part + 1) * HALF)
+            wraps.append(product_of(closed[0][:, columns], closed[1][:, columns], total))
+            wrap_out[:, lanes] = wraps[part]
+        found = []
+        for part, (unused, which, sign, lanes) in enumerate(PARTS):
+            columns = slice(part * HALF, (part + 1) * HALF)
+            gain = (gain_real[:, columns], gain_imag[:, columns])
+            for n in range(TIME):
+                value = product_of(*gain, wraps[part] + sums[n, :, lanes])
+                modes[n, :, lanes] = product_of(
+                    powers[n, 0, :, lanes], powers[n, 1, :, lanes], value
+                )
+            found.append(row_half(modes, table, which, lanes))
+        joined(*found, sent)
 
     return body
 

time: 237 us -> 233 us (0.983)
  Pallas kernels: 26.3 us -> 23 us
    pallas_call x12, Pallas kernels: 26.3 us -> 23 us  [call(): pl.pallas_call(body, out_shape=out_shape, in_specs=[pl.BlockSpec(memory_s...]
  transfers between devices with their start and end apart: 1 -> 1, of which waited for: 0 -> 1; matrix products, arithmetic and copies ran while one was open for 0% -> 0% of each run, Pallas kernels for 0% -> 0%
where the time goes in v4:
time: 233 us; the launch traced here: 232 us
  blocking collectives  205 us (88%)
  Pallas kernels  23 us (10%)
  starting transfers between devices  3.38 us (1%)
    all_to_all x9, blocking collectives, exchange(): lax.all_to_all(value, TM_SPACE, split_axis=0, concat_axis=0, tiled=True)  205 us
    pallas_call x12, Pallas kernels, call(): pl.pallas_call(body, out_shape=out_shape, in_specs=[pl.BlockSpec(memory_s...  23 us
  transfers between devices with their start and end apart: 1, of which 1 were waited for; matrix products, arithmetic and copies ran while one was open for 0% of the time, Pallas kernels for 0%

profile of v4, /device:TPU:1, one launch (start us, length us, event | category | flops | bytes accessed | tf_op | source)
XLA Modules:
  0.0 232.2 jit_solution(12368287883310898813)
XLA Ops:
  0.0 0.0 copy-start.1
  0.0 0.0 copy-start.2
  0.0 0.1 pad_add_fusion
  0.1 0.2 fusion.7
  0.3 0.0 copy-start
  0.3 2.8 %columns.1 = (f32[2,8,256]{2,1,0:T(8,128)S(1)}, f32[2,8,256]{2,1,0:T(8,128)S(1)}) custom-call(f32[2,256,512]{2,1,0:T(8,128)} %far_field.1, f32[256,512]{1,0:T(8,128)} %phase.1, f32[256,512]{1,0:T(8,128)} %absorb.1, f32[16,512]{1,0:T(8,128)S(1)} %pad_maximum_fusion.trig), custom_call_target="tpu_custom_call" | custom-call | tf_op jit(solution)/shard_map/columns/pallas_call | solution.py:73
  3.1 3.4 %collective-permute-start = (f32[2,8,256]{2,1,0:T(8,128)S(1)}, f32[2,8,256]{2,1,0:T(8,128)S(1)}, u32[]{:S(2)}, u32[]{:S(2)}) collective-permute-start(f32[2,8,256]{2,1,0:T(8,128)S(1)} %get-tuple-element.31), channel_id=1, source_target_pairs={{0,5},{1,4},{4,1},{5,0},{2,7},{3,6},{6,3},{7,2},{8,13},{9,12},{12,... | collective-permute-start | bytes 49160 | tf_op jit(solution)/shard_map/ppermute | solution.py:484
  6.5 0.1 multiply_multiply_fusion
  6.5 0.1 pad_maximum_fusion.1
  6.6 0.1 add_multiply_fusion.tangent
  6.7 0.0 copy-done.1
  6.7 0.0 copy-done.2
  6.7 0.3 turning.1.damping
  7.1 0.5 collective-permute-done
  7.6 0.0 copy-done
  7.6 1.7 opening.1
  9.3 30.7 %all_to_all.48.arrived = f32[128,8,256]{2,1,0:T(8,128)S(1)} all-to-all(f32[128,8,256]{2,1,0:T(8,128)S(1)} %get-tuple-element.33), channel_id=1, replica_groups=mesh['tm_0'=4,'tm_1'=4,'tm_2'=2,'tm_3'=2,'space'=2] {'tm_0','tm_1','tm_2..., dimensions={0} | all-to-all | bytes 2097152 | tf_op jit(solution)/shard_map/all_to_all | solution.py:466
  40.0 1.8 cells.4
  41.8 22.9 %all_to_all.49.block = f32[128,8,256]{2,1,0:T(8,128)S(1)} all-to-all(f32[128,8,256]{2,1,0:T(8,128)S(1)} %get-tuple-element.35), channel_id=1, replica_groups=mesh['tm_0'=4,'tm_1'=4,'tm_2'=2,'tm_3'=2,'space'=2] {'tm_0','tm_1','tm_2..., dimensions={0} | all-to-all | bytes 2097152 | tf_op jit(solution)/shard_map/all_to_all | solution.py:466
  64.8 2.4 %modes.3 = (f32[64,8,512]{2,1,0:T(8,128)S(1)}, f32[8,512]{1,0:T(8,128)S(1)}, f32[128,8,256]{2,1,0:T(8,128)S(1)}) custom-call(f32[128,8,256]{2,1,0:T(8,128)S(1)} %all_to_all.49.block, f32[8,512]{1,0:T(8,128)S(1)} %add_multiply_fusion.tangent, bf16[2,3,512,256]{3,2,1,0:T(8,128)(2,1)S(1)} %copy-done, f32[64,2,8,512]{3,2,1,0:T(8,128)S(1)} %get-tuple-element.36.powers, ...), custom_call_target="tpu_custom_call" | custom-call | tf_op jit(solution)/shard_map/modes/pallas_call | solution.py:73
  67.2 22.9 %all_to_all.50.arrived = f32[128,8,256]{2,1,0:T(8,128)S(1)} all-to-all(f32[128,8,256]{2,1,0:T(8,128)S(1)} %get-tuple-element.39), channel_id=1, replica_groups=mesh['tm_0'=4,'tm_1'=4,'tm_2'=2,'tm_3'=2,'space'=2] {'tm_0','tm_1','tm_2..., dimensions={0} | all-to-all | bytes 2097152 | tf_op jit(solution)/shard_map/all_to_all | solution.py:466
  90.1 1.8 cells.5
  92.0 22.9 %all_to_all.51.block = f32[128,8,256]{2,1,0:T(8,128)S(1)} all-to-all(f32[128,8,256]{2,1,0:T(8,128)S(1)} %get-tuple-element.40), channel_id=1, replica_groups=mesh['tm_0'=4,'tm_1'=4,'tm_2'=2,'tm_3'=2,'space'=2] {'tm_0','tm_1','tm_2..., dimensions={0} | all-to-all | bytes 2097152 | tf_op jit(solution)/shard_map/all_to_all | solution.py:466
  114.9 2.5 %modes.4 = (f32[64,8,512]{2,1,0:T(8,128)S(1)}, f32[8,512]{1,0:T(8,128)S(1)}, f32[128,8,256]{2,1,0:T(8,128)S(1)}) custom-call(f32[128,8,256]{2,1,0:T(8,128)S(1)} %all_to_all.51.block, f32[8,512]{1,0:T(8,128)S(1)} %add_multiply_fusion.tangent, bf16[2,3,512,256]{3,2,1,0:T(8,128)(2,1)S(1)} %copy-done, f32[64,2,8,512]{3,2,1,0:T(8,128)S(1)} %get-tuple-element.36.powers, ...), custom_call_target="tpu_custom_call" | custom-call | tf_op jit(solution)/shard_map/modes/pallas_call | solution.py:73
  117.4 22.9 %all_to_all.52.arrived = f32[128,8,256]{2,1,0:T(8,128)S(1)} all-to-all(f32[128,8,256]{2,1,0:T(8,128)S(1)} %get-tuple-element.43), channel_id=1, replica_groups=mesh['tm_0'=4,'tm_1'=4,'tm_2'=2,'tm_3'=2,'space'=2] {'tm_0','tm_1','tm_2..., dimensions={0} | all-to-all | bytes 2097152 | tf_op jit(solution)/shard_map/all_to_all | solution.py:466
  140.3 1.8 cells.6
  142.2 22.9 %all_to_all.53.block = f32[128,8,256]{2,1,0:T(8,128)S(1)} all-to-all(f32[128,8,256]{2,1,0:T(8,128)S(1)} %get-tuple-element.44), channel_id=1, replica_groups=mesh['tm_0'=4,'tm_1'=4,'tm_2'=2,'tm_3'=2,'space'=2] {'tm_0','tm_1','tm_2..., dimensions={0} | all-to-all | bytes 2097152 | tf_op jit(solution)/shard_map/all_to_all | solution.py:466
  165.1 2.5 %modes.5 = (f32[64,8,512]{2,1,0:T(8,128)S(1)}, f32[8,512]{1,0:T(8,128)S(1)}, f32[128,8,256]{2,1,0:T(8,128)S(1)}) custom-call(f32[128,8,256]{2,1,0:T(8,128)S(1)} %all_to_all.53.block, f32[8,512]{1,0:T(8,128)S(1)} %add_multiply_fusion.tangent, bf16[2,3,512,256]{3,2,1,0:T(8,128)(2,1)S(1)} %copy-done, f32[64,2,8,512]{3,2,1,0:T(8,128)S(1)} %get-tuple-element.36.powers, ...), custom_call_target="tpu_custom_call" | custom-call | tf_op jit(solution)/shard_map/modes/pallas_call | solution.py:73
  167.6 22.9 %all_to_all.54.arrived = f32[128,8,256]{2,1,0:T(8,128)S(1)} all-to-all(f32[128,8,256]{2,1,0:T(8,128)S(1)} %get-tuple-element.47), channel_id=1, replica_groups=mesh['tm_0'=4,'tm_1'=4,'tm_2'=2,'tm_3'=2,'space'=2] {'tm_0','tm_1','tm_2..., dimensions={0} | all-to-all | bytes 2097152 | tf_op jit(solution)/shard_map/all_to_all | solution.py:466
  190.5 1.8 cells.7
  192.4 22.9 %all_to_all.55.block = f32[128,8,256]{2,1,0:T(8,128)S(1)} all-to-all(f32[128,8,256]{2,1,0:T(8,128)S(1)} %get-tuple-element.48), channel_id=1, replica_groups=mesh['tm_0'=4,'tm_1'=4,'tm_2'=2,'tm_3'=2,'space'=2] {'tm_0','tm_1','tm_2..., dimensions={0} | all-to-all | bytes 2097152 | tf_op jit(solution)/shard_map/all_to_all | solution.py:466
  215.3 2.0 products.1
  217.3 13.4 %all_to_all.56 = f32[128,1,128]{2,1,0:T(1,128)S(1)} all-to-all(f32[128,1,128]{2,1,0:T(1,128)S(1)} %broadcast_in_dim.2), channel_id=1, replica_groups=mesh['tm_0'=4,'tm_1'=4,'tm_2'=2,'tm_3'=2,'space'=2] {'tm_0','tm_1','tm_2..., dimensions={0} | all-to-all | bytes 131072 | tf_op jit(solution)/shard_map/all_to_all | solution.py:466
  230.7 1.5 combine.1
  (7 shorter events, 0.1 us)
Async XLA Ops:
  0.0 6.7 %copy-start.1 = (f32[256,512]{1,0:T(8,128)S(1)}, f32[256,512]{1,0:T(8,128)}, u32[]{:S(2)}) copy-start(f32[256,512]{1,0:T(8,128)} %phase.1) | copy-start | bytes 1572868
  0.0 6.7 %copy-start.2 = (f32[256,512]{1,0:T(8,128)S(1)}, f32[256,512]{1,0:T(8,128)}, u32[]{:S(2)}) copy-start(f32[256,512]{1,0:T(8,128)} %absorb.1) | copy-start | bytes 1572868
  0.3 7.3 %copy-start = (bf16[2,3,512,256]{3,2,1,0:T(8,128)(2,1)S(1)}, bf16[2,3,512,256]{3,2,1,0:T(8,128)(2,1)}, u32[]{:S(2)}) copy-start(bf16[2,3,512,256]{3,2,1,0:T(8,128)(2,1)} %constant.95.clone.table) | copy-start | bytes 4718596
  3.1 4.5 %collective-permute-start = (f32[2,8,256]{2,1,0:T(8,128)S(1)}, f32[2,8,256]{2,1,0:T(8,128)S(1)}, u32[]{:S(2)}, u32[]{:S(2)}) collective-permute-start(f32[2,8,256]{2,1,0:T(8,128)S(1)} %get-tuple-element.31), channel_id=1, source_target_pairs={{0,5},{1,4},{4,1},{5,0},{2,7},{3,6},{6,3},{7,2},{8,13},{9,12},{12,... | collective-permute-start | bytes 49160 | tf_op jit(solution)/shard_map/ppermute | solution.py:484

commit v5 on v4

--- a/solution.py
+++ b/solution.py
@@ -214,37 +214,34 @@
 NORMAL = 1.0 / (NX * NY)
 
 
-def fetched(sources, targets, arrivals):
-    pieces = []
-    for source, target in zip(sources, targets):
-        for start in range(0, HALF, 64):
-            if len(source.shape) == 3:
-                pieces += [(source.at[c, pl.ds(start, 64)], target.at[c, pl.ds(start, 64)]) for c in range(2)]
-            else:
-                pieces.append((source.at[pl.ds(start, 64)], target.at[pl.ds(start, 64)]))
+def columns_kernel(
+    far_field, far_phase, far_absorb, trig, mine, theirs, field, phase, absorb, arrivals
+):
+    pairs = ((far_field, field), (far_phase, phase), (far_absorb, absorb))
     copies = [
         pltpu.make_async_copy(source, target, arrivals.at[place])
-        for place, (source, target) in enumerate(pieces)
+        for place, (source, target) in enumerate(pairs)
     ]
     for copy in copies:
         copy.start()
-    for copy in copies:
-        copy.wait()
-
-
-def columns_kernel(far_field, far_phase, far_absorb, trig, mine, theirs, field, phase, absorb, arrivals):
-    fetched((far_field, far_phase, far_absorb), (field, phase, absorb), arrivals)
+    trig_high, trig_low = halves(trig[...])
+
+    def transformed(*values):
+        high, low = halves(jnp.concatenate(values, axis=0))
+        return dot_last(trig_high, high) + dot_last(trig_low, high) + dot_last(trig_high, low)
+
+    copies[0].wait()
     real, imag = field[0], field[1]
-    damped_real = 0.5 * (absorb[...] * real - phase[...] * imag)
-    damped_imag = 0.5 * (absorb[...] * imag + phase[...] * real)
-    high, low = halves(jnp.concatenate([real, imag, damped_real, damped_imag], axis=0))
-    trig_high, trig_low = halves(trig[...])
-    product = dot_last(trig_high, high) + dot_last(trig_low, high) + dot_last(trig_high, low)
+    start_product = transformed(real, imag)
+    copies[1].wait()
+    copies[2].wait()
+    damped_product = transformed(
+        0.5 * (absorb[...] * real - phase[...] * imag),
+        0.5 * (absorb[...] * imag + phase[...] * real),
+    )
     upper = upper_rows((8, 1))
-    for place in range(2):
-        start = 2 * place * HALF
-        first = product[:, start : start + HALF]
-        second = product[:, start + HALF : start + 2 * HALF]
+    for place, product in enumerate((start_product, damped_product)):
+        first, second = product[:, :HALF], product[:, HALF:]
         real = first[:8] + second[8:]
         imag = second[:8] - first[8:]
         mine[place] = jnp.where(upper, real, swapped(imag))
@@ -258,7 +255,7 @@
         pltpu.VMEM((2, HALF, NY), f32),
         pltpu.VMEM((HALF, NY), f32),
         pltpu.VMEM((HALF, NY), f32),
-        pltpu.SemaphoreType.DMA((16,)),
+        pltpu.SemaphoreType.DMA((3,)),
     )
     shapes = (array(2, 8, HALF), array(2, 8, HALF))
     return call(columns_kernel, shapes, "columns", scratch, *operands, copied=3)
@@ -285,16 +282,18 @@
     offset[...] = product_of(1.0, slope * side, wrap)
     start = NORMAL * (wrap + value)
 
-    def step(n, power):
-        real, imag = power
-        powers[n, 0] = real
-        powers[n, 1] = imag
-        modes[n] = product_of(real, imag, start)
-        return real * turn_real - imag * turn_imag, real * turn_imag + imag * turn_real
-
-    one = jnp.ones((8, NX), f32)
-    lax.fori_loop(0, TIME, step, (one, jnp.zeros((8, NX), f32)), unroll=4)
-    joined(*[row_half(modes, table, which, lanes) for unused, which, sign, lanes in PARTS], sent)
+    found = []
+    for part, (unused, which, sign, lanes) in enumerate(PARTS):
+        columns = slice(part * HALF, (part + 1) * HALF)
+        turn = turn_real[:, columns], turn_imag[:, columns]
+        real, imag = jnp.ones((8, HALF), f32), jnp.zeros((8, HALF), f32)
+        for n in range(TIME):
+            powers[n, 0, :, lanes] = real
+            powers[n, 1, :, lanes] = imag
+            modes[n, :, lanes] = product_of(real, imag, start[:, columns])
+            real, imag = real * turn[0] - imag * turn[1], real * turn[1] + imag * turn[0]
+        found.append(row_half(modes, table, which, lanes))
+    joined(*found, sent)
 
 
 def opening(block, tangent, table):
@@ -364,26 +363,26 @@
 def products_kernel(block, table, w0, w1, w2, w3, wrap, totals, spectrum):
     rows_forward(block[...], TIME, table, spectrum)
 
-    def narrowed(value):
-        return value[:, 0:128] + value[:, 128:256] + value[:, 256:384] + value[:, 384:512]
-
-    def step(n, carry):
-        before, sums = carry
-        here = spectrum[n]
-        value = here + before - alpha * w3[n]
-        vectors = (None, w1[n], w2[n], w3[n], value)
-        sums = tuple(
-            total + narrowed(vectors[i] * vectors[j]) for total, (i, j) in zip(sums, PAIRS)
-        )
-        return here, sums
-
-    start = w0[...]
-    here = spectrum[0]
-    first = here + (1.0 / scale) * wrap[...] - alpha * w3[0]
-    heads = (start, w1[0], w2[0], w3[0], first)
-    sums = tuple(narrowed(heads[i] * heads[j]) for i, j in PAIRS)
-    unused, sums = lax.fori_loop(1, TIME, step, (here, sums), unroll=3)
-    sums = tuple(narrowed(start * vector) for vector in heads) + sums
+    sums = [None] * (len(PAIRS) + ITERS + 1)
+    order = [(0, j) for j in range(ITERS + 1)] + PAIRS
+
+    def add(place, value):
+        value = value[:, :LANES] + value[:, LANES:]
+        sums[place] = value if sums[place] is None else sums[place] + value
+
+    for part in range(2):
+        lanes = PARTS[part][3]
+        before = (1.0 / scale) * wrap[:, lanes]
+        for n in range(TIME):
+            here = spectrum[n, :, lanes]
+            vectors = [w[n, :, lanes] for w in (w1, w2, w3)]
+            vectors.append(here + before - alpha * vectors[2])
+            vectors.insert(0, w0[:, lanes] if n == 0 else None)
+            before = here
+            for place, (i, j) in enumerate(order):
+                if vectors[i] is not None:
+                    add(place, vectors[i] * vectors[j])
+
     lane = lax.broadcasted_iota(jnp.int32, (1, 128), 1)
     packed = jnp.zeros((1, 128), f32)
     for place, total in enumerate(sums):

time: 233 us -> 232 us (level)
  no operation moved by 1% of the time
where the time goes in v5:
time: 232 us; the launch traced here: 231 us
  blocking collectives  205 us (88%)
  Pallas kernels  22.2 us (10%)
  starting transfers between devices  3.38 us (1%)
    all_to_all x9, blocking collectives, exchange(): lax.all_to_all(value, TM_SPACE, split_axis=0, concat_axis=0, tiled=True)  205 us
    pallas_call x12, Pallas kernels, call(): pl.pallas_call(body, out_shape=out_shape, in_specs=[pl.BlockSpec(memory_s...  22.2 us
  transfers between devices with their start and end apart: 1, of which 1 were waited for; matrix products, arithmetic and copies ran while one was open for 0% of the time, Pallas kernels for 0%

profile of v5, /device:TPU:1, one launch (start us, length us, event | category | flops | bytes accessed | tf_op | source)
XLA Modules:
  0.0 231.4 jit_solution(5035165495447550868)
XLA Ops:
  0.0 0.0 copy-start.1
  0.0 0.0 copy-start.2
  0.0 0.1 pad_add_fusion
  0.1 0.2 fusion.7
  0.3 0.0 copy-start
  0.3 2.5 %columns.1 = (f32[2,8,256]{2,1,0:T(8,128)S(1)}, f32[2,8,256]{2,1,0:T(8,128)S(1)}) custom-call(f32[2,256,512]{2,1,0:T(8,128)} %far_field.1, f32[256,512]{1,0:T(8,128)} %phase.1, f32[256,512]{1,0:T(8,128)} %absorb.1, f32[16,512]{1,0:T(8,128)S(1)} %pad_maximum_fusion.trig), custom_call_target="tpu_custom_call" | custom-call | tf_op jit(solution)/shard_map/columns/pallas_call | solution.py:73
  2.7 3.4 %collective-permute-start = (f32[2,8,256]{2,1,0:T(8,128)S(1)}, f32[2,8,256]{2,1,0:T(8,128)S(1)}, u32[]{:S(2)}, u32[]{:S(2)}) collective-permute-start(f32[2,8,256]{2,1,0:T(8,128)S(1)} %get-tuple-element.31), channel_id=1, source_target_pairs={{0,5},{1,4},{4,1},{5,0},{2,7},{3,6},{6,3},{7,2},{8,13},{9,12},{12,... | collective-permute-start | bytes 49160 | tf_op jit(solution)/shard_map/ppermute | solution.py:483
  6.1 0.1 multiply_multiply_fusion
  6.2 0.1 pad_maximum_fusion.1
  6.3 0.1 add_multiply_fusion.tangent
  6.4 0.0 copy-done.1
  6.4 0.0 copy-done.2
  6.4 0.3 turning.1.damping
  6.7 0.5 collective-permute-done
  7.3 0.0 copy-done
  7.3 1.4 opening.1
  8.7 30.7 %all_to_all.48.arrived = f32[128,8,256]{2,1,0:T(8,128)S(1)} all-to-all(f32[128,8,256]{2,1,0:T(8,128)S(1)} %get-tuple-element.33), channel_id=1, replica_groups=mesh['tm_0'=4,'tm_1'=4,'tm_2'=2,'tm_3'=2,'space'=2] {'tm_0','tm_1','tm_2..., dimensions={0} | all-to-all | bytes 2097152 | tf_op jit(solution)/shard_map/all_to_all | solution.py:465
  39.5 1.8 cells.4
  41.3 22.9 %all_to_all.49.block = f32[128,8,256]{2,1,0:T(8,128)S(1)} all-to-all(f32[128,8,256]{2,1,0:T(8,128)S(1)} %get-tuple-element.35), channel_id=1, replica_groups=mesh['tm_0'=4,'tm_1'=4,'tm_2'=2,'tm_3'=2,'space'=2] {'tm_0','tm_1','tm_2..., dimensions={0} | all-to-all | bytes 2097152 | tf_op jit(solution)/shard_map/all_to_all | solution.py:465
  64.2 2.4 %modes.3 = (f32[64,8,512]{2,1,0:T(8,128)S(1)}, f32[8,512]{1,0:T(8,128)S(1)}, f32[128,8,256]{2,1,0:T(8,128)S(1)}) custom-call(f32[128,8,256]{2,1,0:T(8,128)S(1)} %all_to_all.49.block, f32[8,512]{1,0:T(8,128)S(1)} %add_multiply_fusion.tangent, bf16[2,3,512,256]{3,2,1,0:T(8,128)(2,1)S(1)} %copy-done, f32[64,2,8,512]{3,2,1,0:T(8,128)S(1)} %get-tuple-element.36.powers, ...), custom_call_target="tpu_custom_call" | custom-call | tf_op jit(solution)/shard_map/modes/pallas_call | solution.py:73
  66.7 22.9 %all_to_all.50.arrived = f32[128,8,256]{2,1,0:T(8,128)S(1)} all-to-all(f32[128,8,256]{2,1,0:T(8,128)S(1)} %get-tuple-element.39), channel_id=1, replica_groups=mesh['tm_0'=4,'tm_1'=4,'tm_2'=2,'tm_3'=2,'space'=2] {'tm_0','tm_1','tm_2..., dimensions={0} | all-to-all | bytes 2097152 | tf_op jit(solution)/shard_map/all_to_all | solution.py:465
  89.6 1.8 cells.5
  91.4 22.9 %all_to_all.51.block = f32[128,8,256]{2,1,0:T(8,128)S(1)} all-to-all(f32[128,8,256]{2,1,0:T(8,128)S(1)} %get-tuple-element.40), channel_id=1, replica_groups=mesh['tm_0'=4,'tm_1'=4,'tm_2'=2,'tm_3'=2,'space'=2] {'tm_0','tm_1','tm_2..., dimensions={0} | all-to-all | bytes 2097152 | tf_op jit(solution)/shard_map/all_to_all | solution.py:465
  114.4 2.5 %modes.4 = (f32[64,8,512]{2,1,0:T(8,128)S(1)}, f32[8,512]{1,0:T(8,128)S(1)}, f32[128,8,256]{2,1,0:T(8,128)S(1)}) custom-call(f32[128,8,256]{2,1,0:T(8,128)S(1)} %all_to_all.51.block, f32[8,512]{1,0:T(8,128)S(1)} %add_multiply_fusion.tangent, bf16[2,3,512,256]{3,2,1,0:T(8,128)(2,1)S(1)} %copy-done, f32[64,2,8,512]{3,2,1,0:T(8,128)S(1)} %get-tuple-element.36.powers, ...), custom_call_target="tpu_custom_call" | custom-call | tf_op jit(solution)/shard_map/modes/pallas_call | solution.py:73
  116.8 22.9 %all_to_all.52.arrived = f32[128,8,256]{2,1,0:T(8,128)S(1)} all-to-all(f32[128,8,256]{2,1,0:T(8,128)S(1)} %get-tuple-element.43), channel_id=1, replica_groups=mesh['tm_0'=4,'tm_1'=4,'tm_2'=2,'tm_3'=2,'space'=2] {'tm_0','tm_1','tm_2..., dimensions={0} | all-to-all | bytes 2097152 | tf_op jit(solution)/shard_map/all_to_all | solution.py:465
  139.8 1.8 cells.6
  141.6 22.9 %all_to_all.53.block = f32[128,8,256]{2,1,0:T(8,128)S(1)} all-to-all(f32[128,8,256]{2,1,0:T(8,128)S(1)} %get-tuple-element.44), channel_id=1, replica_groups=mesh['tm_0'=4,'tm_1'=4,'tm_2'=2,'tm_3'=2,'space'=2] {'tm_0','tm_1','tm_2..., dimensions={0} | all-to-all | bytes 2097152 | tf_op jit(solution)/shard_map/all_to_all | solution.py:465
  164.6 2.5 %modes.5 = (f32[64,8,512]{2,1,0:T(8,128)S(1)}, f32[8,512]{1,0:T(8,128)S(1)}, f32[128,8,256]{2,1,0:T(8,128)S(1)}) custom-call(f32[128,8,256]{2,1,0:T(8,128)S(1)} %all_to_all.53.block, f32[8,512]{1,0:T(8,128)S(1)} %add_multiply_fusion.tangent, bf16[2,3,512,256]{3,2,1,0:T(8,128)(2,1)S(1)} %copy-done, f32[64,2,8,512]{3,2,1,0:T(8,128)S(1)} %get-tuple-element.36.powers, ...), custom_call_target="tpu_custom_call" | custom-call | tf_op jit(solution)/shard_map/modes/pallas_call | solution.py:73
  167.0 22.9 %all_to_all.54.arrived = f32[128,8,256]{2,1,0:T(8,128)S(1)} all-to-all(f32[128,8,256]{2,1,0:T(8,128)S(1)} %get-tuple-element.47), channel_id=1, replica_groups=mesh['tm_0'=4,'tm_1'=4,'tm_2'=2,'tm_3'=2,'space'=2] {'tm_0','tm_1','tm_2..., dimensions={0} | all-to-all | bytes 2097152 | tf_op jit(solution)/shard_map/all_to_all | solution.py:465
  190.0 1.8 cells.7
  191.8 22.9 %all_to_all.55.block = f32[128,8,256]{2,1,0:T(8,128)S(1)} all-to-all(f32[128,8,256]{2,1,0:T(8,128)S(1)} %get-tuple-element.48), channel_id=1, replica_groups=mesh['tm_0'=4,'tm_1'=4,'tm_2'=2,'tm_3'=2,'space'=2] {'tm_0','tm_1','tm_2..., dimensions={0} | all-to-all | bytes 2097152 | tf_op jit(solution)/shard_map/all_to_all | solution.py:465
  214.7 1.7 products.1
  216.5 0.1 broadcast_in_dim.2
  216.5 13.4 %all_to_all.56 = f32[128,1,128]{2,1,0:T(1,128)S(1)} all-to-all(f32[128,1,128]{2,1,0:T(1,128)S(1)} %broadcast_in_dim.2), channel_id=1, replica_groups=mesh['tm_0'=4,'tm_1'=4,'tm_2'=2,'tm_3'=2,'space'=2] {'tm_0','tm_1','tm_2..., dimensions={0} | all-to-all | bytes 131072 | tf_op jit(solution)/shard_map/all_to_all | solution.py:465
  229.9 1.5 combine.1
  (6 shorter events, 0.1 us)
Async XLA Ops:
  0.0 6.4 %copy-start.1 = (f32[256,512]{1,0:T(8,128)S(1)}, f32[256,512]{1,0:T(8,128)}, u32[]{:S(2)}) copy-start(f32[256,512]{1,0:T(8,128)} %phase.1) | copy-start | bytes 1572868
  0.0 6.4 %copy-start.2 = (f32[256,512]{1,0:T(8,128)S(1)}, f32[256,512]{1,0:T(8,128)}, u32[]{:S(2)}) copy-start(f32[256,512]{1,0:T(8,128)} %absorb.1) | copy-start | bytes 1572868
  0.3 7.0 %copy-start = (bf16[2,3,512,256]{3,2,1,0:T(8,128)(2,1)S(1)}, bf16[2,3,512,256]{3,2,1,0:T(8,128)(2,1)}, u32[]{:S(2)}) copy-start(bf16[2,3,512,256]{3,2,1,0:T(8,128)(2,1)} %constant.95.clone.table) | copy-start | bytes 4718596
  2.7 4.5 %collective-permute-start = (f32[2,8,256]{2,1,0:T(8,128)S(1)}, f32[2,8,256]{2,1,0:T(8,128)S(1)}, u32[]{:S(2)}, u32[]{:S(2)}) collective-permute-start(f32[2,8,256]{2,1,0:T(8,128)S(1)} %get-tuple-element.31), channel_id=1, source_target_pairs={{0,5},{1,4},{4,1},{5,0},{2,7},{3,6},{6,3},{7,2},{8,13},{9,12},{12,... | collective-permute-start | bytes 49160 | tf_op jit(solution)/shard_map/ppermute | solution.py:483

commit v6 on v5

--- a/solution.py
+++ b/solution.py
@@ -270,7 +270,27 @@
     return call(turning_kernel, array(2, NY, HALF), "turning", (), phase, absorb)
 
 
-def opening_kernel(block, tangent, table, vector, offset, sent, powers, spectrum, modes):
+def tables_kernel(tangent, powers, ramps, closed):
+    turn_real, turn_imag, gain_real, gain_imag = rotation(tangent[...])
+    closed[0], closed[1] = closing((turn_real, turn_imag))
+    power = jnp.ones((8, NX), f32), jnp.zeros((8, NX), f32)
+    ramp = NORMAL * gain_real, NORMAL * gain_imag
+    for n in range(TIME):
+        for target, (real, imag) in ((powers, power), (ramps, ramp)):
+            target[n, 0] = real
+            target[n, 1] = imag
+        power, ramp = [
+            (real * turn_real - imag * turn_imag, real * turn_imag + imag * turn_real)
+            for real, imag in (power, ramp)
+        ]
+
+
+def power_tables(tangent):
+    shapes = (array(TIME, 2, 8, NX), array(TIME, 2, 8, NX), array(2, 8, NX))
+    return call(tables_kernel, shapes, "tables", (), tangent)
+
+
+def opening_kernel(block, tangent, table, powers, closed, vector, wrap_out, sent, spectrum, modes):
     rows_forward(block[...], 2, table, spectrum)
     slope = tangent[...]
     turn_real, turn_imag, gain_real, gain_imag = rotation(slope)
@@ -278,45 +298,33 @@
     wave, damped = spectrum[0], spectrum[1]
     vector[...] = product_of(1.0, -slope * side, wave) - damped
     value = product_of(turn_real, turn_imag, wave) - product_of(gain_real, gain_imag, damped)
-    wrap = product_of(*closing((turn_real, turn_imag)), value)
-    offset[...] = product_of(1.0, slope * side, wrap)
+    wrap = product_of(closed[0], closed[1], value)
+    wrap_out[...] = product_of(1.0, slope * side, wrap)
     start = NORMAL * (wrap + value)
-
     found = []
     for part, (unused, which, sign, lanes) in enumerate(PARTS):
-        columns = slice(part * HALF, (part + 1) * HALF)
-        turn = turn_real[:, columns], turn_imag[:, columns]
-        real, imag = jnp.ones((8, HALF), f32), jnp.zeros((8, HALF), f32)
+        here = start[:, part * HALF : (part + 1) * HALF]
         for n in range(TIME):
-            powers[n, 0, :, lanes] = real
-            powers[n, 1, :, lanes] = imag
-            modes[n, :, lanes] = product_of(real, imag, start[:, columns])
-            real, imag = real * turn[0] - imag * turn[1], real * turn[1] + imag * turn[0]
+            modes[n, :, lanes] = product_of(powers[n, 0, :, lanes], powers[n, 1, :, lanes], here)
         found.append(row_half(modes, table, which, lanes))
     joined(*found, sent)
 
 
-def opening(block, tangent, table):
-    shapes = (
-        array(8, NX),
-        array(8, NX),
-        array(DEVICES, 8, HALF),
-        array(TIME, 2, 8, NX),
-    )
+def opening(block, tangent, table, powers, closed):
+    shapes = (array(8, NX), array(8, NX), array(DEVICES, 8, HALF))
     scratch = (pltpu.VMEM((2, 8, NX), f32), pltpu.VMEM((TIME, 8, NX), f32))
-    return call(opening_kernel, shapes, "opening", scratch, block, tangent, table)
+    operands = (block, tangent, table, powers, closed)
+    return call(opening_kernel, shapes, "opening", scratch, *operands)
 
 
 def modes_kernel_of(first):
-    def body(block, tangent, table, powers, earlier, wrap_in, vector, wrap_out, sent, modes, sums):
+    def body(
+        block, table, powers, ramps, closed, earlier, wrap_in, vector, wrap_out, sent, modes, sums
+    ):
         rows_forward(block[...], TIME, table, modes)
-        slope = tangent[...]
-        turn_real, turn_imag, gain_real, gain_imag = rotation(slope)
         start = (1.0 / scale) * wrap_in[...]
         if first:
             start = start - alpha * earlier[...]
-        closed = closing((turn_real, turn_imag))
-        gain_real, gain_imag = NORMAL * gain_real, NORMAL * gain_imag
         wraps = []
         for part in range(2):
             lanes = PARTS[part][3]
@@ -329,19 +337,16 @@
                 if not first:
                     value = value - alpha * earlier[n, :, lanes]
                 vector[n, :, lanes] = value
-                total = total + product_of(powers[n, 0, :, lanes], -powers[n, 1, :, lanes], value)
+                real, imag = powers[n, 0, :, lanes], powers[n, 1, :, lanes]
+                total = total + (real * value - imag * swapped(value))
                 sums[n, :, lanes] = total
-            columns = slice(part * HALF, (part + 1) * HALF)
-            wraps.append(product_of(closed[0][:, columns], closed[1][:, columns], total))
+            wraps.append(product_of(closed[0, :, lanes], closed[1, :, lanes], total))
             wrap_out[:, lanes] = wraps[part]
         found = []
         for part, (unused, which, sign, lanes) in enumerate(PARTS):
-            columns = slice(part * HALF, (part + 1) * HALF)
-            gain = (gain_real[:, columns], gain_imag[:, columns])
             for n in range(TIME):
-                value = product_of(*gain, wraps[part] + sums[n, :, lanes])
                 modes[n, :, lanes] = product_of(
-                    powers[n, 0, :, lanes], powers[n, 1, :, lanes], value
+                    ramps[n, 0, :, lanes], ramps[n, 1, :, lanes], wraps[part] + sums[n, :, lanes]
                 )
             found.append(row_half(modes, table, which, lanes))
         joined(*found, sent)
@@ -349,11 +354,11 @@
     return body
 
 
-def on_modes(block, tangent, table, powers, earlier, wrap, first):
+def on_modes(block, table, tables, earlier, wrap, first):
     shapes = (array(TIME, 8, NX), array(8, NX), array(DEVICES, 8, HALF))
     scratch = (pltpu.VMEM((TIME, 8, NX), f32), pltpu.VMEM((TIME, 8, NX), f32))
     body = modes_kernel_of(first)
-    operands = (block, tangent, table, powers, earlier, wrap)
+    operands = (block, table, *tables, earlier, wrap)
     return call(body, shapes, "modes", scratch, *operands)
 
 
@@ -491,9 +496,11 @@
     symbol_x = 4.0 * jnp.sin(rows * (math.pi / NX)) ** 2
     tangent = (0.5 * tau) * (jnp.concatenate([symbol_y, symbol_y])[:, None] + symbol_x[None, :])
     damping = turned(phase, absorb)
-    block, damping = lax.optimization_barrier((block, damping))
-
-    vector, wrap, sent, powers = opening(block, tangent, table)
+    tables = power_tables(tangent)
+    block, damping, tables = lax.optimization_barrier((block, damping, tables))
+
+    powers, ramps, closed = tables
+    vector, wrap, sent = opening(block, tangent, table, powers, closed)
     vectors = [vector]
     found = []
     for column in range(ITERS):
@@ -502,7 +509,7 @@
         arrived = exchange(sent)
         if column + 1 < ITERS:
             vector, wrap, sent = on_modes(
-                arrived, tangent, table, powers, vectors[-1], wrap, column == 0
+                arrived, table, tables, vectors[-1], wrap, column == 0
             )
             vectors.append(vector)
     totals = products(arrived, table, vectors, wrap)

time: 232 us -> 231 us (level)
    pallas_call x12 -> x13, Pallas kernels: 22.2 us -> 21.7 us  [call(): pl.pallas_call(body, out_shape=out_shape, in_specs=[pl.BlockSpec(memory_s...]
  transfers between devices with their start and end apart: 1 -> 1, of which waited for: 1 -> 0; matrix products, arithmetic and copies ran while one was open for 0% -> 0% of each run, Pallas kernels for 0% -> 0%
where the time goes in v6:
time: 231 us; the launch traced here: 230 us
  blocking collectives  205 us (89%)
  Pallas kernels  21.7 us (9%)
  starting transfers between devices  3.38 us (1%)
    all_to_all x9, blocking collectives, exchange(): lax.all_to_all(value, TM_SPACE, split_axis=0, concat_axis=0, tiled=True)  205 us
    pallas_call x13, Pallas kernels, call(): pl.pallas_call(body, out_shape=out_shape, in_specs=[pl.BlockSpec(memory_s...  21.7 us
  transfers between devices with their start and end apart: 1, of which 0 were waited for; matrix products, arithmetic and copies ran while one was open for 0% of the time, Pallas kernels for 0%

profile of v6, /device:TPU:1, one launch (start us, length us, event | category | flops | bytes accessed | tf_op | source)
XLA Modules:
  0.0 230.5 jit_solution(3357649561915734453)
XLA Ops:
  0.0 0.0 copy-start.1
  0.0 0.0 copy-start.2
  0.0 0.1 pad_add_fusion
  0.1 0.2 fusion.7
  0.3 0.0 copy-start
  0.3 2.5 %columns.1 = (f32[2,8,256]{2,1,0:T(8,128)S(1)}, f32[2,8,256]{2,1,0:T(8,128)S(1)}) custom-call(f32[2,256,512]{2,1,0:T(8,128)} %far_field.1, f32[256,512]{1,0:T(8,128)} %phase.1, f32[256,512]{1,0:T(8,128)} %absorb.1, f32[16,512]{1,0:T(8,128)S(1)} %pad_maximum_fusion.trig), custom_call_target="tpu_custom_call" | custom-call | tf_op jit(solution)/shard_map/columns/pallas_call | solution.py:73
  2.7 3.4 %collective-permute-start = (f32[2,8,256]{2,1,0:T(8,128)S(1)}, f32[2,8,256]{2,1,0:T(8,128)S(1)}, u32[]{:S(2)}, u32[]{:S(2)}) collective-permute-start(f32[2,8,256]{2,1,0:T(8,128)S(1)} %get-tuple-element.36), channel_id=1, source_target_pairs={{0,5},{1,4},{4,1},{5,0},{2,7},{3,6},{6,3},{7,2},{8,13},{9,12},{12,... | collective-permute-start | bytes 49160 | tf_op jit(solution)/shard_map/ppermute | solution.py:488
  6.1 0.1 multiply_multiply_fusion
  6.2 0.1 pad_maximum_fusion.1
  6.3 0.1 add_multiply_fusion.tangent
  6.4 0.0 copy-done.1
  6.4 0.0 copy-done.2
  6.4 0.3 turning.1.damping
  6.7 0.5 tables.1
  7.2 0.0 collective-permute-done
  7.3 0.0 copy-done
  7.3 1.3 opening.1
  8.6 30.7 %all_to_all.48.arrived = f32[128,8,256]{2,1,0:T(8,128)S(1)} all-to-all(f32[128,8,256]{2,1,0:T(8,128)S(1)} %get-tuple-element.43), channel_id=1, replica_groups=mesh['tm_0'=4,'tm_1'=4,'tm_2'=2,'tm_3'=2,'space'=2] {'tm_0','tm_1','tm_2..., dimensions={0} | all-to-all | bytes 2097152 | tf_op jit(solution)/shard_map/all_to_all | solution.py:470
  39.3 1.8 cells.4
  41.2 22.9 %all_to_all.49.block = f32[128,8,256]{2,1,0:T(8,128)S(1)} all-to-all(f32[128,8,256]{2,1,0:T(8,128)S(1)} %get-tuple-element.45), channel_id=1, replica_groups=mesh['tm_0'=4,'tm_1'=4,'tm_2'=2,'tm_3'=2,'space'=2] {'tm_0','tm_1','tm_2..., dimensions={0} | all-to-all | bytes 2097152 | tf_op jit(solution)/shard_map/all_to_all | solution.py:470
  64.1 2.1 modes.3
  66.2 22.9 %all_to_all.50.arrived = f32[128,8,256]{2,1,0:T(8,128)S(1)} all-to-all(f32[128,8,256]{2,1,0:T(8,128)S(1)} %get-tuple-element.49), channel_id=1, replica_groups=mesh['tm_0'=4,'tm_1'=4,'tm_2'=2,'tm_3'=2,'space'=2] {'tm_0','tm_1','tm_2..., dimensions={0} | all-to-all | bytes 2097152 | tf_op jit(solution)/shard_map/all_to_all | solution.py:470
  89.2 1.8 cells.5
  91.0 22.9 %all_to_all.51.block = f32[128,8,256]{2,1,0:T(8,128)S(1)} all-to-all(f32[128,8,256]{2,1,0:T(8,128)S(1)} %get-tuple-element.50), channel_id=1, replica_groups=mesh['tm_0'=4,'tm_1'=4,'tm_2'=2,'tm_3'=2,'space'=2] {'tm_0','tm_1','tm_2..., dimensions={0} | all-to-all | bytes 2097152 | tf_op jit(solution)/shard_map/all_to_all | solution.py:470
  113.9 2.2 modes.4
  116.1 22.9 %all_to_all.52.arrived = f32[128,8,256]{2,1,0:T(8,128)S(1)} all-to-all(f32[128,8,256]{2,1,0:T(8,128)S(1)} %get-tuple-element.53), channel_id=1, replica_groups=mesh['tm_0'=4,'tm_1'=4,'tm_2'=2,'tm_3'=2,'space'=2] {'tm_0','tm_1','tm_2..., dimensions={0} | all-to-all | bytes 2097152 | tf_op jit(solution)/shard_map/all_to_all | solution.py:470
  139.1 1.8 cells.6
  140.9 22.9 %all_to_all.53.block = f32[128,8,256]{2,1,0:T(8,128)S(1)} all-to-all(f32[128,8,256]{2,1,0:T(8,128)S(1)} %get-tuple-element.54), channel_id=1, replica_groups=mesh['tm_0'=4,'tm_1'=4,'tm_2'=2,'tm_3'=2,'space'=2] {'tm_0','tm_1','tm_2..., dimensions={0} | all-to-all | bytes 2097152 | tf_op jit(solution)/shard_map/all_to_all | solution.py:470
  163.8 2.2 modes.5
  166.0 22.9 %all_to_all.54.arrived = f32[128,8,256]{2,1,0:T(8,128)S(1)} all-to-all(f32[128,8,256]{2,1,0:T(8,128)S(1)} %get-tuple-element.57), channel_id=1, replica_groups=mesh['tm_0'=4,'tm_1'=4,'tm_2'=2,'tm_3'=2,'space'=2] {'tm_0','tm_1','tm_2..., dimensions={0} | all-to-all | bytes 2097152 | tf_op jit(solution)/shard_map/all_to_all | solution.py:470
  189.0 1.8 cells.7
  190.8 22.9 %all_to_all.55.block = f32[128,8,256]{2,1,0:T(8,128)S(1)} all-to-all(f32[128,8,256]{2,1,0:T(8,128)S(1)} %get-tuple-element.58), channel_id=1, replica_groups=mesh['tm_0'=4,'tm_1'=4,'tm_2'=2,'tm_3'=2,'space'=2] {'tm_0','tm_1','tm_2..., dimensions={0} | all-to-all | bytes 2097152 | tf_op jit(solution)/shard_map/all_to_all | solution.py:470
  213.7 1.7 products.1
  215.5 0.1 broadcast_in_dim.2
  215.5 13.4 %all_to_all.56 = f32[128,1,128]{2,1,0:T(1,128)S(1)} all-to-all(f32[128,1,128]{2,1,0:T(1,128)S(1)} %broadcast_in_dim.2), channel_id=1, replica_groups=mesh['tm_0'=4,'tm_1'=4,'tm_2'=2,'tm_3'=2,'space'=2] {'tm_0','tm_1','tm_2..., dimensions={0} | all-to-all | bytes 131072 | tf_op jit(solution)/shard_map/all_to_all | solution.py:470
  228.9 1.6 combine.1
  (6 shorter events, 0.1 us)
Async XLA Ops:
  0.0 6.4 %copy-start.1 = (f32[256,512]{1,0:T(8,128)S(1)}, f32[256,512]{1,0:T(8,128)}, u32[]{:S(2)}) copy-start(f32[256,512]{1,0:T(8,128)} %phase.1) | copy-start | bytes 1572868
  0.0 6.4 %copy-start.2 = (f32[256,512]{1,0:T(8,128)S(1)}, f32[256,512]{1,0:T(8,128)}, u32[]{:S(2)}) copy-start(f32[256,512]{1,0:T(8,128)} %absorb.1) | copy-start | bytes 1572868
  0.3 7.0 %copy-start = (bf16[2,3,512,256]{3,2,1,0:T(8,128)(2,1)S(1)}, bf16[2,3,512,256]{3,2,1,0:T(8,128)(2,1)}, u32[]{:S(2)}) copy-start(bf16[2,3,512,256]{3,2,1,0:T(8,128)(2,1)} %constant.95.clone.table) | copy-start | bytes 4718596
  2.7 4.5 %collective-permute-start = (f32[2,8,256]{2,1,0:T(8,128)S(1)}, f32[2,8,256]{2,1,0:T(8,128)S(1)}, u32[]{:S(2)}, u32[]{:S(2)}) collective-permute-start(f32[2,8,256]{2,1,0:T(8,128)S(1)} %get-tuple-element.36), channel_id=1, source_target_pairs={{0,5},{1,4},{4,1},{5,0},{2,7},{3,6},{6,3},{7,2},{8,13},{9,12},{12,... | collective-permute-start | bytes 49160 | tf_op jit(solution)/shard_map/ppermute | solution.py:488

commit v7 on v6

--- a/solution.py
+++ b/solution.py
@@ -444,7 +444,7 @@
     return factors
 
 
-def combine_kernel(totals, z0, z1, z2, z3, out):
+def combine_kernel(totals, z0, z1, z2, z3, out, result, departures):
     summed = jnp.sum(totals[...], axis=0, keepdims=True)
     size = ITERS + 1
     gram = [[None] * size for unused in range(size)]
@@ -455,15 +455,34 @@
         gram[i][j] = value
         gram[j][i] = value
     factors = least_squares(gram)
+    copies = []
     for part in range(2):
-        value = factors[0] * z0[part]
-        for factor, other in zip(factors[1:], (z1, z2, z3)):
-            value = value + factor * other[part]
-        out[part, 0] = value.T
+        for place in range(2):
+            rows = pl.ds(place * LANES, LANES)
+            value = factors[0] * z0[part, :, rows]
+            for factor, other in zip(factors[1:], (z1, z2, z3)):
+                value = value + factor * other[part, :, rows]
+            result[part, rows] = value.T
+            copy = pltpu.make_async_copy(
+                result.at[part, rows], out.at[part, 0, rows], departures.at[2 * part + place]
+            )
+            copy.start()
+            copies.append(copy)
+    for copy in copies:
+        copy.wait()
 
 
 def combine(totals, fields):
-    return call(combine_kernel, array(2, 1, HALF, NY), "combine", (), totals, *fields)
+    inside = pl.BlockSpec(memory_space=pltpu.VMEM)
+    return pl.pallas_call(
+        combine_kernel,
+        out_shape=array(2, 1, HALF, NY),
+        in_specs=[inside] * 5,
+        out_specs=pl.BlockSpec(memory_space=pltpu.HBM),
+        scratch_shapes=(pltpu.VMEM((2, HALF, NY), f32), pltpu.SemaphoreType.DMA((4,))),
+        compiler_params=pltpu.CompilerParams(vmem_limit_bytes=24 << 20),
+        name="combine",
+    )(totals, *fields)
 
 
 def exchange(value):

time: 231 us -> 231 us (level)
    pallas_call x13 -> x12, Pallas kernels: 21.7 us -> 20.1 us  [call(): pl.pallas_call(body, out_shape=out_shape, in_specs=[pl.BlockSpec(memory_s...]
where the time goes in v7:
time: 231 us; the launch traced here: 230 us
  blocking collectives  205 us (89%)
  Pallas kernels  21.5 us (9%)
  starting transfers between devices  3.38 us (1%)
    all_to_all x9, blocking collectives, exchange(): lax.all_to_all(value, TM_SPACE, split_axis=0, concat_axis=0, tiled=True)  205 us
    pallas_call x12, Pallas kernels, call(): pl.pallas_call(body, out_shape=out_shape, in_specs=[pl.BlockSpec(memory_s...  20.1 us
  transfers between devices with their start and end apart: 1, of which 0 were waited for; matrix products, arithmetic and copies ran while one was open for 0% of the time, Pallas kernels for 0%

profile of v7, /device:TPU:1, one launch (start us, length us, event | category | flops | bytes accessed | tf_op | source)
XLA Modules:
  0.0 230.4 jit_solution(14834604290439997049)
XLA Ops:
  0.0 0.0 copy-start.1
  0.0 0.0 copy-start.2
  0.0 0.1 pad_add_fusion
  0.1 0.2 fusion.7
  0.3 0.0 copy-start
  0.3 2.5 %columns.1 = (f32[2,8,256]{2,1,0:T(8,128)S(1)}, f32[2,8,256]{2,1,0:T(8,128)S(1)}) custom-call(f32[2,256,512]{2,1,0:T(8,128)} %far_field.1, f32[256,512]{1,0:T(8,128)} %phase.1, f32[256,512]{1,0:T(8,128)} %absorb.1, f32[16,512]{1,0:T(8,128)S(1)} %pad_maximum_fusion.trig), custom_call_target="tpu_custom_call" | custom-call | tf_op jit(solution)/shard_map/columns/pallas_call | solution.py:73
  2.7 3.4 %collective-permute-start = (f32[2,8,256]{2,1,0:T(8,128)S(1)}, f32[2,8,256]{2,1,0:T(8,128)S(1)}, u32[]{:S(2)}, u32[]{:S(2)}) collective-permute-start(f32[2,8,256]{2,1,0:T(8,128)S(1)} %get-tuple-element.36), channel_id=1, source_target_pairs={{0,5},{1,4},{4,1},{5,0},{2,7},{3,6},{6,3},{7,2},{8,13},{9,12},{12,... | collective-permute-start | bytes 49160 | tf_op jit(solution)/shard_map/ppermute | solution.py:507
  6.1 0.1 multiply_multiply_fusion
  6.2 0.1 pad_maximum_fusion.1
  6.3 0.1 add_multiply_fusion.tangent
  6.4 0.0 copy-done.1
  6.4 0.0 copy-done.2
  6.4 0.3 turning.1.damping
  6.7 0.5 tables.1
  7.2 0.0 collective-permute-done
  7.3 0.0 copy-done
  7.3 1.3 opening.1
  8.6 30.7 %all_to_all.48.arrived = f32[128,8,256]{2,1,0:T(8,128)S(1)} all-to-all(f32[128,8,256]{2,1,0:T(8,128)S(1)} %get-tuple-element.43), channel_id=1, replica_groups=mesh['tm_0'=4,'tm_1'=4,'tm_2'=2,'tm_3'=2,'space'=2] {'tm_0','tm_1','tm_2..., dimensions={0} | all-to-all | bytes 2097152 | tf_op jit(solution)/shard_map/all_to_all | solution.py:489
  39.3 1.8 cells.4
  41.2 22.9 %all_to_all.49.block = f32[128,8,256]{2,1,0:T(8,128)S(1)} all-to-all(f32[128,8,256]{2,1,0:T(8,128)S(1)} %get-tuple-element.45), channel_id=1, replica_groups=mesh['tm_0'=4,'tm_1'=4,'tm_2'=2,'tm_3'=2,'space'=2] {'tm_0','tm_1','tm_2..., dimensions={0} | all-to-all | bytes 2097152 | tf_op jit(solution)/shard_map/all_to_all | solution.py:489
  64.1 2.1 modes.3
  66.2 22.9 %all_to_all.50.arrived = f32[128,8,256]{2,1,0:T(8,128)S(1)} all-to-all(f32[128,8,256]{2,1,0:T(8,128)S(1)} %get-tuple-element.49), channel_id=1, replica_groups=mesh['tm_0'=4,'tm_1'=4,'tm_2'=2,'tm_3'=2,'space'=2] {'tm_0','tm_1','tm_2..., dimensions={0} | all-to-all | bytes 2097152 | tf_op jit(solution)/shard_map/all_to_all | solution.py:489
  89.2 1.8 cells.5
  91.0 22.9 %all_to_all.51.block = f32[128,8,256]{2,1,0:T(8,128)S(1)} all-to-all(f32[128,8,256]{2,1,0:T(8,128)S(1)} %get-tuple-element.50), channel_id=1, replica_groups=mesh['tm_0'=4,'tm_1'=4,'tm_2'=2,'tm_3'=2,'space'=2] {'tm_0','tm_1','tm_2..., dimensions={0} | all-to-all | bytes 2097152 | tf_op jit(solution)/shard_map/all_to_all | solution.py:489
  113.9 2.2 modes.4
  116.1 22.9 %all_to_all.52.arrived = f32[128,8,256]{2,1,0:T(8,128)S(1)} all-to-all(f32[128,8,256]{2,1,0:T(8,128)S(1)} %get-tuple-element.53), channel_id=1, replica_groups=mesh['tm_0'=4,'tm_1'=4,'tm_2'=2,'tm_3'=2,'space'=2] {'tm_0','tm_1','tm_2..., dimensions={0} | all-to-all | bytes 2097152 | tf_op jit(solution)/shard_map/all_to_all | solution.py:489
  139.1 1.8 cells.6
  140.9 22.9 %all_to_all.53.block = f32[128,8,256]{2,1,0:T(8,128)S(1)} all-to-all(f32[128,8,256]{2,1,0:T(8,128)S(1)} %get-tuple-element.54), channel_id=1, replica_groups=mesh['tm_0'=4,'tm_1'=4,'tm_2'=2,'tm_3'=2,'space'=2] {'tm_0','tm_1','tm_2..., dimensions={0} | all-to-all | bytes 2097152 | tf_op jit(solution)/shard_map/all_to_all | solution.py:489
  163.8 2.2 modes.5
  166.0 22.9 %all_to_all.54.arrived = f32[128,8,256]{2,1,0:T(8,128)S(1)} all-to-all(f32[128,8,256]{2,1,0:T(8,128)S(1)} %get-tuple-element.57), channel_id=1, replica_groups=mesh['tm_0'=4,'tm_1'=4,'tm_2'=2,'tm_3'=2,'space'=2] {'tm_0','tm_1','tm_2..., dimensions={0} | all-to-all | bytes 2097152 | tf_op jit(solution)/shard_map/all_to_all | solution.py:489
  189.0 1.8 cells.7
  190.8 22.9 %all_to_all.55.block = f32[128,8,256]{2,1,0:T(8,128)S(1)} all-to-all(f32[128,8,256]{2,1,0:T(8,128)S(1)} %get-tuple-element.58), channel_id=1, replica_groups=mesh['tm_0'=4,'tm_1'=4,'tm_2'=2,'tm_3'=2,'space'=2] {'tm_0','tm_1','tm_2..., dimensions={0} | all-to-all | bytes 2097152 | tf_op jit(solution)/shard_map/all_to_all | solution.py:489
  213.7 1.7 products.1
  215.5 0.1 broadcast_in_dim.2
  215.5 13.4 %all_to_all.56 = f32[128,1,128]{2,1,0:T(1,128)S(1)} all-to-all(f32[128,1,128]{2,1,0:T(1,128)S(1)} %broadcast_in_dim.2), channel_id=1, replica_groups=mesh['tm_0'=4,'tm_1'=4,'tm_2'=2,'tm_3'=2,'space'=2] {'tm_0','tm_1','tm_2..., dimensions={0} | all-to-all | bytes 131072 | tf_op jit(solution)/shard_map/all_to_all | solution.py:489
  228.9 1.4 combine.1
  (6 shorter events, 0.1 us)
Async XLA Ops:
  0.0 6.4 %copy-start.1 = (f32[256,512]{1,0:T(8,128)S(1)}, f32[256,512]{1,0:T(8,128)}, u32[]{:S(2)}) copy-start(f32[256,512]{1,0:T(8,128)} %phase.1) | copy-start | bytes 1572868
  0.0 6.4 %copy-start.2 = (f32[256,512]{1,0:T(8,128)S(1)}, f32[256,512]{1,0:T(8,128)}, u32[]{:S(2)}) copy-start(f32[256,512]{1,0:T(8,128)} %absorb.1) | copy-start | bytes 1572868
  0.3 7.0 %copy-start = (bf16[2,3,512,256]{3,2,1,0:T(8,128)(2,1)S(1)}, bf16[2,3,512,256]{3,2,1,0:T(8,128)(2,1)}, u32[]{:S(2)}) copy-start(bf16[2,3,512,256]{3,2,1,0:T(8,128)(2,1)} %constant.95.clone.table) | copy-start | bytes 4718596
  2.7 4.5 %collective-permute-start = (f32[2,8,256]{2,1,0:T(8,128)S(1)}, f32[2,8,256]{2,1,0:T(8,128)S(1)}, u32[]{:S(2)}, u32[]{:S(2)}) collective-permute-start(f32[2,8,256]{2,1,0:T(8,128)S(1)} %get-tuple-element.36), channel_id=1, source_target_pairs={{0,5},{1,4},{4,1},{5,0},{2,7},{3,6},{6,3},{7,2},{8,13},{9,12},{12,... | collective-permute-start | bytes 49160 | tf_op jit(solution)/shard_map/ppermute | solution.py:507
